TPU v7x, 128 devices: a whole 4x4x4 slice. The times are simulated.
128 devices in a mesh: rep: 1, dp: 128 (over x, y, z, core).
Axes of the slice: x: 4, y: 4, z: 4, core: 2. Of those that a mesh axis runs over, the one named last changes fastest.
Arguments:
- x: bfloat16 [128, 2048, 1024], P(('rep', 'dp'))
- dy: bfloat16 [128, 2048, 1024], P(('rep', 'dp'))
- w_gate: bfloat16 [2, 1024, 2816], P(None, 'dp')
- w_up: bfloat16 [2, 1024, 2816], P(None, 'dp')
- w_down: bfloat16 [2, 2816, 1024], P(None, 'dp')
Outputs:
- output 1: bfloat16 [128, 2048, 1024], P(('rep', 'dp'))
- output 2: bfloat16 [2, 1024, 2816], P('rep', 'dp')
- output 3: bfloat16 [2, 1024, 2816], P('rep', 'dp')
- output 4: bfloat16 [2, 2816, 1024], P('rep', 'dp')
All inputs are finite; a program needn't handle non-finite values.
Results may differ from a plain program's by a relative error of at most 0.018.
Values are sent between devices in bfloat16 or wider.
A program may use at most 1.5 GiB of HBM per device.

v0:
```python
import jax
import jax.numpy as jnp
from jax import lax

NAMES = ("w_gate", "w_up", "w_down")


def matmul(a, w):
    return jnp.dot(a, w, preferred_element_type=jnp.float32).astype(jnp.bfloat16)


def normed(h):
    wide = h.astype(jnp.float32)
    scale = lax.rsqrt(jnp.mean(wide**2, -1, keepdims=True) + 1e-6)
    return (wide * scale).astype(jnp.bfloat16)


def layer(h, w):
    a = normed(h)
    gate = jnp.dot(a, w["w_gate"], preferred_element_type=jnp.float32)
    up = jnp.dot(a, w["w_up"], preferred_element_type=jnp.float32)
    return h + matmul((jax.nn.silu(gate) * up).astype(jnp.bfloat16), w["w_down"])


def stack(weights, h):
    for number in range(weights["w_gate"].shape[0]):
        h = layer(h, {name: w[number] for name, w in weights.items()})
    return h


def solution(mesh):
    groups = mesh.shape["rep"]

    def step(x, dy, *weights):
        shape = x.shape
        x, dy = (t.reshape(groups, -1, *t.shape[1:]) for t in (x, dy))

        def of_a_group(x, dy):
            _, back = jax.vjp(stack, dict(zip(NAMES, weights, strict=True)), x)
            by_weights, by_x = back(dy)
            return (by_x, *(by_weights[name] for name in NAMES))

        by_x, *by_weights = jax.vmap(of_a_group)(x, dy)
        return (by_x.reshape(shape), *(t.reshape(-1, *t.shape[2:]) for t in by_weights))

    return step
```

profile of v0, /device:TPU:0, one launch (start us, length us, event | category | flops | bytes accessed | tf_op | source)
XLA Modules:
  0.0 3085.5 jit_solution(7779529618769573345)
XLA Ops:
  10.2 1.8 fusion.102
  13.9 6.6 copy.13
  20.4 3.1 fusion.38
  24.1 6.4 copy.14
  30.6 50.7 %all-gather.29.cloned.1.call-done = bf16[1,1024,2816]{2,1,0:T(8,128)(2,1)} async-done(((bf16[1,8,2816]{2,1,0:T(8,128)(2,1)}), bf16[1,1024,2816]{2,1,0:T(8,128)(2,1)}) %all-gather.29.cloned.1.call-update) | async-done | bytes 5767184 | tf_op jit(solution)/vmap(jvp())/squeeze | solution.py:27
  81.2 20.0 fusion.61
  101.2 48.2 %all-gather.31.cloned.1.call-done = bf16[1,1024,2816]{2,1,0:T(8,128)(2,1)} async-done(((bf16[1,8,2816]{2,1,0:T(8,128)(2,1)}), bf16[1,1024,2816]{2,1,0:T(8,128)(2,1)}) %all-gather.31.cloned.1.call-update) | async-done | bytes 5767184 | tf_op jit(solution)/vmap(jvp())/squeeze | solution.py:27
  149.4 20.5 fusion.57
  169.9 19.7 fusion.26
  189.6 32.8 %all-gather.33.cloned.1.call-done = bf16[1,2816,1024]{2,0,1:T(2,128)(2,1)} async-done(((bf16[1,22,1024]{2,0,1:T(2,128)(2,1)}), bf16[1,2816,1024]{2,0,1:T(2,128)(2,1)}) %all-gather.33.cloned.1.call-update) | async-done | bytes 5767184 | tf_op jit(solution)/vmap(jvp())/squeeze | solution.py:27
  222.4 22.5 fusion.41
  245.5 51.2 %all-gather.37.cloned.1.call-done = bf16[1,2816,1024]{2,0,1:T(2,128)(2,1)} async-done(((bf16[1,22,1024]{2,0,1:T(2,128)(2,1)}), bf16[1,2816,1024]{2,0,1:T(2,128)(2,1)}) %all-gather.37.cloned.1.call-update) | async-done | bytes 5767184 | tf_op jit(solution)/vmap(jvp())/squeeze | solution.py:27
  296.7 19.9 convolution_convert_fusion.1
  316.6 49.6 %all-gather.35.cloned.1.call-done = bf16[1,1024,2816]{2,1,0:T(8,128)(2,1)} async-done(((bf16[1,8,2816]{2,1,0:T(8,128)(2,1)}), bf16[1,1024,2816]{2,1,0:T(8,128)(2,1)}) %all-gather.35.cloned.1.call-update) | async-done | bytes 5767184 | tf_op jit(solution)/vmap(jvp())/squeeze | solution.py:27
  366.2 20.0 fusion.54
  386.3 21.6 fusion.22
  408.0 26.9 all-gather.39.cloned.1.call-done
  434.8 19.9 fusion.49
  454.7 23.3 fusion.6
  478.0 21.6 fusion.24
  499.6 18.9 fusion.43
  518.6 4.6 fusion.66
  523.2 20.4 convolution_convert_fusion
  543.6 21.2 fusion.18
  564.9 20.0 fusion.9
  584.9 4.2 copy-done.5
  589.0 14.9 fusion.79
  604.0 19.1 fusion.84
  623.1 19.0 fusion.67
  642.1 24.4 fusion.28
  666.5 368.5 %fusion.97 = (f32[1024,24]{0,1:T(8,128)S(1)}, f32[24,1024]{1,0:T(8,128)S(1)}) fusion(f32[1024,2816]{0,1:T(8,128)} %fusion.67, f32[2816,1024]{1,0:T(8,128)} %fusion.28), kind=kCustom, calls=%all-reduce-scatter.2 | all-reduce-scatter fusion | flops 6291457 | bytes 23265280
  1042.8 4.2 collective-permute-start.5
  1047.0 21.5 fusion.20
  1074.3 1.9 collective-permute-start
  1076.2 19.0 fusion.40
  1097.0 3.0 collective-permute-start.13
  1100.0 2.5 collective-permute-start.14
  1102.5 3.9 collective-permute-start.15
  1110.9 8.8 collective-permute-start.19
  1119.7 22.5 collective-permute-start.20
  1142.2 2.6 collective-permute-start.11
  1144.8 4.7 fusion.65
  1149.5 6.4 copy.15
  1155.9 1.8 concatenate
  1157.7 1.8 concatenate.1
  1161.3 598.3 %reduce-scatter.25.cloned.1.call-done = f32[2816,8]{0,1:T(8,128)} async-done(((f32[2816,1024]{0,1:T(8,128)}), f32[2816,8]{0,1:T(8,128)}) %reduce-scatter.25.cloned.1.call-update) | async-done | bytes 90128
  1761.1 657.1 %reduce-scatter.21.cloned.1.call-done = f32[2816,8]{0,1:T(8,128)} async-done(((f32[2816,1024]{0,1:T(8,128)}), f32[2816,8]{0,1:T(8,128)}) %reduce-scatter.21.cloned.1.call-update) | async-done | bytes 90128
  2419.1 657.6 %reduce-scatter.19.cloned.1.call-done = f32[2816,8]{0,1:T(8,128)} async-done(((f32[2816,1024]{0,1:T(8,128)}), f32[2816,8]{0,1:T(8,128)}) %reduce-scatter.19.cloned.1.call-update) | async-done | bytes 90128
  (110 shorter events, 31.6 us)
Async XLA Ops:
  7.2 74.1 %all-gather.29.cloned.1.call-start = ((), (), s32[]{:S(2)}) async-start(), calls=%async_computation.4 | async-start | bytes 5812224 | tf_op jit(solution)/vmap(jvp())/squeeze | solution.py:27
  8.7 140.7 %all-gather.31.cloned.1.call-start = ((), (), s32[]{:S(2)}) async-start(), calls=%async_computation.5 | async-start | bytes 5812224 | tf_op jit(solution)/vmap(jvp())/squeeze | solution.py:27
  10.2 212.2 %all-gather.33.cloned.1.call-start = ((), (), s32[]{:S(2)}) async-start(), calls=%async_computation.6 | async-start | bytes 11624448 | tf_op jit(solution)/vmap(jvp())/squeeze | solution.py:27
  12.1 284.7 %all-gather.37.cloned.1.call-start = ((), (), s32[]{:S(2)}) async-start(), calls=%async_computation.8 | async-start | bytes 11624448 | tf_op jit(solution)/vmap(jvp())/squeeze | solution.py:27
  12.6 353.6 %all-gather.35.cloned.1.call-start = ((), (), s32[]{:S(2)}) async-start(), calls=%async_computation.7 | async-start | bytes 5812224 | tf_op jit(solution)/vmap(jvp())/squeeze | solution.py:27
  13.2 421.6 %all-gather.39.cloned.1.call-start = ((), (), s32[]{:S(2)}) async-start(), calls=%async_computation.9 | async-start | bytes 5812224 | tf_op jit(solution)/vmap(jvp())/squeeze | solution.py:27
  13.8 1146.5 %reduce-scatter.23.cloned.1.call-start = ((), (), s32[]{:S(2)}) async-start(), calls=%async_computation.12 | async-start | bytes 11624448
  23.5 0.6 copy-start.9
  24.1 125.3 %copy-start.13 = (f32[1,2048]{1,0:T(1,128)}, f32[1,2048]{1,0:T(1,128)S(1)}, u32[]{:S(2)}) copy-start(f32[1,2048]{1,0:T(1,128)S(1)} %rsqrt.22) | copy-start | bytes 24580
  244.9 0.6 copy-start.11
  366.2 20.1 copy-start.6
  407.9 1351.7 %reduce-scatter.25.cloned.1.call-start = ((), (), s32[]{:S(2)}) async-start(), calls=%async_computation.13 | async-start | bytes 11624448
  499.6 18.9 copy-start.12
  499.6 19.0 copy-start.4
  499.6 19.0 copy-start.7
  523.2 20.4 copy-start
  523.2 20.4 copy-start.14
  564.8 1853.4 %reduce-scatter.21.cloned.1.call-start = ((), (), s32[]{:S(2)}) async-start(), calls=%async_computation.11 | async-start | bytes 11624448
  564.9 24.2 copy-start.1
  584.8 4.2 copy-start.5
  604.0 2472.7 %reduce-scatter.19.cloned.1.call-start = ((), (), s32[]{:S(2)}) async-start(), calls=%async_computation.10 | async-start | bytes 11624448
  623.1 19.0 copy-start.8
  1035.0 6.5 collective-permute-start.10
  1036.3 6.5 collective-permute-start.21
  1037.6 30.9 %collective-permute-start.1 = (bf16[24,1024]{1,0:T(8,128)(2,1)S(1)}, bf16[24,1024]{1,0:T(8,128)(2,1)S(1)}, u32[]{:S(2)}, u32[]{:S(2)}) collective-permute-start(bf16[24,1024]{1,0:T(8,128)(2,1)S(1)} %convert.82), channel_id=1, source_target_pairs={{0,2},{1,3},{2,4},{3,5},{4,6},{5,7},{6,8},{7,9},{8,10},{9,11},{10,... | collective-permute-start | bytes 147464
  1038.9 31.1 %collective-permute-start.2 = (bf16[24,1024]{1,0:T(8,128)(2,1)S(1)}, bf16[24,1024]{1,0:T(8,128)(2,1)S(1)}, u32[]{:S(2)}, u32[]{:S(2)}) collective-permute-start(bf16[24,1024]{1,0:T(8,128)(2,1)S(1)} %convert.82), channel_id=1, source_target_pairs={{0,3},{1,4},{2,5},{3,6},{4,7},{5,8},{6,9},{7,10},{8,11},{9,12},{10... | collective-permute-start | bytes 147464
  1040.2 31.4 %collective-permute-start.3 = (bf16[24,1024]{1,0:T(8,128)(2,1)S(1)}, bf16[24,1024]{1,0:T(8,128)(2,1)S(1)}, u32[]{:S(2)}, u32[]{:S(2)}) collective-permute-start(bf16[24,1024]{1,0:T(8,128)(2,1)S(1)} %convert.82), channel_id=1, source_target_pairs={{0,4},{1,5},{2,6},{3,7},{4,8},{5,9},{6,10},{7,11},{8,12},{9,13},{1... | collective-permute-start | bytes 147464
  1041.5 31.4 %collective-permute-start.4 = (bf16[24,1024]{1,0:T(8,128)(2,1)S(1)}, bf16[24,1024]{1,0:T(8,128)(2,1)S(1)}, u32[]{:S(2)}, u32[]{:S(2)}) collective-permute-start(bf16[24,1024]{1,0:T(8,128)(2,1)S(1)} %convert.82), channel_id=1, source_target_pairs={{0,5},{1,6},{2,7},{3,8},{4,9},{5,10},{6,11},{7,12},{8,13},{9,14},{... | collective-permute-start | bytes 147464
  1042.8 31.4 %collective-permute-start.5 = (bf16[24,1024]{1,0:T(8,128)(2,1)S(1)}, bf16[24,1024]{1,0:T(8,128)(2,1)S(1)}, u32[]{:S(2)}, u32[]{:S(2)}) collective-permute-start(bf16[24,1024]{1,0:T(8,128)(2,1)S(1)} %convert.82), channel_id=1, source_target_pairs={{0,6},{1,7},{2,8},{3,9},{4,10},{5,11},{6,12},{7,13},{8,14},{9,15},... | collective-permute-start | bytes 147464
  1068.5 39.4 %copy-start.10 = (f32[2048]{0:T(1024)S(1)}, f32[2048]{0:T(1024)}, u32[]{:S(2)}) copy-start(f32[2048]{0:T(1024)} %copy-done.9) | copy-start | bytes 24580
  1068.5 76.3 %copy-start.2 = (bf16[1,2048,1024]{1,2,0:T(8,128)(2,1)S(1)}, bf16[1,2048,1024]{1,2,0:T(8,128)(2,1)}, u32[]{:S(2)}) copy-start(bf16[1,2048,1024]{1,2,0:T(8,128)(2,1)} %copy.13) | copy-start | bytes 12582916
  1068.5 76.3 %copy-start.3 = (bf16[1,2048,1024]{1,2,0:T(8,128)(2,1)S(1)}, bf16[1,2048,1024]{1,2,0:T(8,128)(2,1)}, u32[]{:S(2)}) copy-start(bf16[1,2048,1024]{1,2,0:T(8,128)(2,1)} %fusion.66) | copy-start | bytes 12582916
  1068.5 76.3 %copy-start.15 = (f32[1,2048]{1,0:T(1,128)S(1)}, f32[1,2048]{1,0:T(1,128)}, u32[]{:S(2)}) copy-start(f32[1,2048]{1,0:T(1,128)} %copy-done.13) | copy-start | bytes 24580
  1068.5 26.7 collective-permute-start.6
  1070.1 26.9 collective-permute-start.7
  1071.6 28.3 collective-permute-start.8
  1073.0 29.5 collective-permute-start.9
  1074.3 32.2 %collective-permute-start = (bf16[24,1024]{1,0:T(8,128)(2,1)S(1)}, bf16[24,1024]{1,0:T(8,128)(2,1)S(1)}, u32[]{:S(2)}, u32[]{:S(2)}) collective-permute-start(bf16[24,1024]{1,0:T(8,128)(2,1)S(1)} %convert.82), channel_id=1, source_target_pairs={{0,1},{1,2},{2,3},{3,4},{4,5},{5,6},{6,7},{7,8},{8,9},{9,10},{10,1... | collective-permute-start | bytes 147464
  1095.2 12.7 collective-permute-start.12
  1097.0 12.6 collective-permute-start.13
  1100.0 10.9 collective-permute-start.14
  1102.5 17.2 collective-permute-start.15
  1106.5 35.7 %collective-permute-start.16 = (bf16[1024,24]{0,1:T(8,128)(2,1)S(1)}, bf16[1024,24]{0,1:T(8,128)(2,1)S(1)}, u32[]{:S(2)}, u32[]{:S(2)}) collective-permute-start(bf16[1024,24]{0,1:T(8,128)(2,1)S(1)} %convert.83), channel_id=1, source_target_pairs={{0,6},{1,7},{2,8},{3,9},{4,10},{5,11},{6,12},{7,13},{8,14},{9,15},... | collective-permute-start | bytes 147464
  1107.9 49.8 %collective-permute-start.17 = (bf16[1024,24]{0,1:T(8,128)(2,1)S(1)}, bf16[1024,24]{0,1:T(8,128)(2,1)S(1)}, u32[]{:S(2)}, u32[]{:S(2)}) collective-permute-start(bf16[1024,24]{0,1:T(8,128)(2,1)S(1)} %convert.83), channel_id=1, source_target_pairs={{0,7},{1,8},{2,9},{3,10},{4,11},{5,12},{6,13},{7,14},{8,15},{9,16}... | collective-permute-start | bytes 147464
  1109.5 48.1 %collective-permute-start.18 = (bf16[1024,24]{0,1:T(8,128)(2,1)S(1)}, bf16[1024,24]{0,1:T(8,128)(2,1)S(1)}, u32[]{:S(2)}, u32[]{:S(2)}) collective-permute-start(bf16[1024,24]{0,1:T(8,128)(2,1)S(1)} %convert.83), channel_id=1, source_target_pairs={{0,8},{1,9},{2,10},{3,11},{4,12},{5,13},{6,14},{7,15},{8,16},{9,17... | collective-permute-start | bytes 147464
  1110.9 46.8 %collective-permute-start.19 = (bf16[1024,24]{0,1:T(8,128)(2,1)S(1)}, bf16[1024,24]{0,1:T(8,128)(2,1)S(1)}, u32[]{:S(2)}, u32[]{:S(2)}) collective-permute-start(bf16[1024,24]{0,1:T(8,128)(2,1)S(1)} %convert.83), channel_id=1, source_target_pairs={{0,9},{1,10},{2,11},{3,12},{4,13},{5,14},{6,15},{7,16},{8,17},{9,1... | collective-permute-start | bytes 147464
  1119.7 38.0 %collective-permute-start.20 = (bf16[1024,24]{0,1:T(8,128)(2,1)S(1)}, bf16[1024,24]{0,1:T(8,128)(2,1)S(1)}, u32[]{:S(2)}, u32[]{:S(2)}) collective-permute-start(bf16[1024,24]{0,1:T(8,128)(2,1)S(1)} %convert.83), channel_id=1, source_target_pairs={{0,10},{1,11},{2,12},{3,13},{4,14},{5,15},{6,16},{7,17},{8,18},{9,... | collective-permute-start | bytes 147464
  1142.2 15.5 collective-permute-start.11
Sparse Core Ops, SparseCore 0:
  11.0 70.2 all-gather.28
  84.2 65.1 all-gather.30
  152.9 69.3 all-gather.32
  225.8 70.9 all-gather.36
  299.6 66.6 all-gather.34
  369.6 65.1 all-gather.38
  437.2 663.6 reduce-scatter.22
  1103.2 656.2 reduce-scatter.24
  1761.9 656.1 reduce-scatter.20
  2420.4 656.1 reduce-scatter.18
where the time goes:
time: 3090 us
  waiting for transfers between devices  2170 us (70%)
  blocking collectives  368 us (12%)
  matrix products  344 us (11%)
  other arithmetic  80.2 us (3%)
  starting transfers between devices  69.3 us (2%)
  local copies, waits for them, and re-layouts  33.9 us (1%)
    unnamed x36, waiting for transfers between devices  1910 us
    unnamed x1, blocking collectives  368 us
    squeeze x6, waiting for transfers between devices, stack(): h = layer(h, {name: w[number] for name, w in weights.items()})  259 us
    dot_general x6, matrix products, layer(): up = jnp.dot(a, w['w_up'], preferred_element_type=jnp.float32)  126 us
    dot_general x6, matrix products, layer(): gate = jnp.dot(a, w['w_gate'], preferred_element_type=jnp.float32)  112 us
    dot_general x5, matrix products, matmul(): jnp.dot(a, w, preferred_element_type=jnp.float32).astype(jnp.bfloat16)  106 us
    unnamed x26, starting transfers between devices  69 us
    unnamed x5, other arithmetic  62.9 us
  transfers between devices with their start and end apart: 32, of which 9 were waited for; matrix products, arithmetic and copies ran while one was open for 27% of the time, Pallas kernels for 0%

commit v1 on v0

v1 whole, which is shorter than its diff:
```python
import functools

import jax
import jax.numpy as jnp
from jax import lax
from jax.experimental import pallas as pl
from jax.experimental.pallas import tpu as pltpu
from jax.sharding import PartitionSpec as P

bf=jnp.bfloat16
RING=4
COLS=256
LANES=128
ROWS=22
PAD=24
GROUP=8*ROWS
ALLOF=...
f32=jnp.float32
SUB=COLS
MESH=pl.DeviceIdType.MESH
W=8
ORDERS=((2,1,0),(0,2,1),(1,0,2))

def coords():
    me=lax.axis_index("dp")
    return (me//32, (me//8)%RING, (me//2)%RING), me%2

def dev(xyz,c):
    return {"dp": ((xyz[0]*RING+xyz[1])*RING+xyz[2])*2+c}

def moved(xyz,axis,to):
    return tuple(to if k==axis else v for k,v in enumerate(xyz))

def region(g,item,full,xyz,c,rows=slice(None),cols=slice(None)):
    ix=tuple(slice(None) if k in full else xyz[k] for k in range(3))
    return g.at[(item,*ix,c,rows,cols)]

def entry_barrier():
    xyz,c=coords()
    b=pltpu.get_barrier_semaphore()
    n=0
    for axis in range(3):
        for d in (1,2,3):
            pl.semaphore_signal(b,inc=1,device_id=dev(moved(xyz,axis,(xyz[axis]+d)%RING),c),device_id_type=MESH)
            n+=1
    pl.semaphore_signal(b,inc=1,device_id=dev(xyz,1-c),device_id_type=MESH)
    pl.semaphore_wait(b,n+1)

class Gather:
    STAGES=7
    def __init__(self,order,g,own,send,recv,local,halves):
        self.order,self.g,self.own,self.send,self.recv,self.local,self.halves=order,g,own,send,recv,local,halves
    def copies(self,stage,item):
        xyz,c=coords()
        a,b,last=self.order
        g=self.g
        slot=item%W
        sigma=1-2*c
        def copy(k,src,dst,to,tc=None):
            return pltpu.make_async_remote_copy(src_ref=src,dst_ref=dst,send_sem=self.send.at[slot,k],recv_sem=self.recv.at[slot,k],
                device_id=dev(to,c if tc is None else tc),device_id_type=MESH)
        if stage==0:
            mine=region(g,item,(),xyz,c)
            out=[copy(d-1,self.own(item),mine,moved(xyz,a,(xyz[a]+d)%RING)) for d in (1,2,3)]
            return out
        if stage in (1,3):
            axis,full=(b,(a,)) if stage==1 else (last,(a,b))
            r=region(g,item,full,xyz,c)
            k=3 if stage==1 else 7
            p,q=(xyz[axis]+sigma+RING)%RING,(xyz[axis]-sigma+RING)%RING
            return [copy(k,r,r,moved(xyz,axis,p)),copy(k+1,r,r,moved(xyz,axis,q))]
        if stage in (2,RING):
            axis,full=(b,(a,)) if stage==2 else (last,(a,b))
            k=5 if stage==2 else 9
            p,q=(xyz[axis]+sigma+RING)%RING,(xyz[axis]-sigma+RING)%RING
            (ra,ca),(rb,cb)=self.halves
            fromq=region(g,item,full,moved(xyz,axis,q),c,ra,ca)
            fromp=region(g,item,full,moved(xyz,axis,p),c,rb,cb)
            return [copy(k,fromq,fromq,moved(xyz,axis,p)),copy(k+1,fromp,fromp,moved(xyz,axis,q))]
        if stage==5:
            r=region(g,item,(0,1,2),xyz,c)
            return [copy(11,r,r,xyz,1-c)]
    def own_copy(self,item):
        xyz,c=coords()
        return pltpu.make_async_copy(self.own(item),region(self.g,item,(),xyz,c),self.local.at[item%W])
    def run(self,stage,item):
        if stage>0:
            for cp in self.copies(stage-1,item): cp.wait()
            if stage==1: self.own_copy(item).wait()
        if stage<6:
            for cp in self.copies(stage,item): cp.start()
            if stage==0: self.own_copy(item).start()

def ag_kernel(items,counts,wg,wu,wd,gg,gu,gd,wdp,*sems):
    L=wd.shape[0]
    wdp[ALLOF]=jnp.zeros_like(wdp)
    for l in range(L):
        wdp[l,0:ROWS,:]=wd[l]
    entry_barrier()
    ng,nd=counts
    half_c=((slice(None),pl.ds(0,LANES)),(slice(None),pl.ds(LANES,LANES)))
    half_r=((pl.ds(0,16),slice(None)),(pl.ds(16,8),slice(None)))
    own_g=lambda i: wg.at[i//ng,:,pl.ds(pl.multiple_of(i%ng*COLS,COLS),COLS)]
    own_u=lambda i: wu.at[i//ng,:,pl.ds(pl.multiple_of(i%ng*COLS,COLS),COLS)]
    own_d=lambda i: wdp.at[i//nd,:,pl.ds(pl.multiple_of(i%nd*LANES,LANES),LANES)]
    eg=Gather(ORDERS[0],gg,own_g,*sems[0:3],half_c)
    eu=Gather(ORDERS[1],gu,own_u,*sems[3:6],half_c)
    ed=Gather(ORDERS[2],gd,own_d,*sems[6:9],half_r)
    def tick(t,carry):
        for stage in reversed(range(7)):
            i=t-stage
            @pl.when((i>=0)&(i<items))
            def _():
                eg.run(stage,i); eu.run(stage,i)
                @pl.when(i%ng<nd)
                def _():
                    ed.run(stage,i//ng*nd+i%ng)
        return carry
    lax.fori_loop(0,items+6,tick,0)

def gather(wg,wu,wd):
    L,_,F=wg.shape; D=wd.shape[2]
    ng,nd=F//COLS,D//LANES
    assert nd<=ng or L==1
    items=L*ng
    sem=pltpu.SemaphoreType.DMA
    f=pl.pallas_call(functools.partial(ag_kernel,items,(ng,nd)),
        out_shape=[jax.ShapeDtypeStruct((L*ng,RING,RING,RING,2,8,COLS),bf)]*2+[jax.ShapeDtypeStruct((L*nd,RING,RING,RING,2,PAD,LANES),bf)],
        in_specs=[pl.BlockSpec(memory_space=pltpu.VMEM)]*3,
        out_specs=[pl.BlockSpec(memory_space=pl.ANY)]*3,
        scratch_shapes=[pltpu.VMEM((L,PAD,D),bf)]+[sem((W,12)),sem((W,12)),sem((W,))]*3,
        compiler_params=pltpu.CompilerParams(collective_id=0,has_side_effects=True),name="gather")
    return tuple(f(wg,wu,wd))

ALL=slice(None)
class Scatter:
    STAGES=7
    TW=RING
    @staticmethod
    def scratch(R,n,halves):
        (ra,ca),(rb,cb)=halves
        V=lambda *s: pltpu.VMEM(s,bf)
        return dict(ds=V(2,RING,RING,RING,R,n),dr=V(RING,RING,RING,RING,R,n),
            a1s=V(2,RING,RING,R,n),a1A=V(2,RING,RING,ra.size,ca.size),a1B=V(2,RING,RING,rb.size,cb.size),
            a2s=V(2,2,RING,RING,R,n),a2r=V(2,2,RING,RING,R,n),t1=pltpu.VMEM((2,RING,RING,R,n),f32),
            b1s=V(2,RING,R,n),b1A=V(2,RING,ra.size,ca.size),b1B=V(2,RING,rb.size,cb.size),
            b2s=V(2,2,RING,R,n),b2r=V(2,2,RING,R,n),t2=pltpu.VMEM((2,RING,R,n),f32),
            cs=V(2,3,R,n),cr=V(2,3,R,n),
            send=pltpu.SemaphoreType.DMA((2,12)),recv=pltpu.SemaphoreType.DMA((2,12)))
    def __init__(self,order,term,out,halves,refs):
        self.order,self.term,self.out,self.halves=order,term,out,halves
        self.__dict__.update(refs)
    def geometry(self):
        xyz,c=coords()
        cx,b,a=self.order
        sigma=1-2*c
        return xyz,c,a,b,cx,sigma
    def copies(self,stage,item):
        xyz,c,a,b,cx,sigma=self.geometry()
        s=item%2
        def copy(k,src,dst,to,tc=None):
            return pltpu.make_async_remote_copy(src_ref=src,dst_ref=dst,send_sem=self.send.at[s,k],recv_sem=self.recv.at[s,k],
                device_id=dev(to,c if tc is None else tc),device_id_type=MESH)
        if stage==0: return [copy(0,self.ds.at[s],self.dr.at[item%RING],xyz,1-c)]
        if stage in (1,3):
            axis=a if stage==1 else b
            k,src,A,B=(1,self.a1s,self.a1A,self.a1B) if stage==1 else (5,self.b1s,self.b1A,self.b1B)
            lead=(ALL,)*(2 if stage==1 else 1)
            p,q=(xyz[axis]+sigma+RING)%RING,(xyz[axis]-sigma+RING)%RING
            (ra,ca),(rb,cb)=self.halves
            return [copy(k,src.at[(s,*lead,ra,ca)],A.at[s],moved(xyz,axis,p)),copy(k+1,src.at[(s,*lead,rb,cb)],B.at[s],moved(xyz,axis,q))]
        if stage in (2,RING):
            axis=a if stage==2 else b
            k,src,dst=(3,self.a2s,self.a2r) if stage==2 else (7,self.b2s,self.b2r)
            p,q=(xyz[axis]+sigma+RING)%RING,(xyz[axis]-sigma+RING)%RING
            return [copy(k,src.at[s,0],dst.at[s,0],moved(xyz,axis,p)),copy(k+1,src.at[s,1],dst.at[s,1],moved(xyz,axis,q))]
        if stage==5:
            return [copy(8+d,self.cs.at[s,d-1],self.cr.at[s,d-1],moved(xyz,cx,(xyz[cx]+d)%RING)) for d in (1,2,3)]
    def run(self,stage,item):
        xyz,c,a,b,cx,sigma=self.geometry()
        s=item%2
        ts=item%self.TW; d4=item%RING
        (ra,ca),(rb,cb)=self.halves
        if stage>0:
            for cp in self.copies(stage-1,item): cp.wait()
        def plane(v):
            ix=tuple(v if k==a else ALL for k in range(3))
            return self.term[(ts,*ix,c)]+self.dr[(d4,*ix)].astype(f32)
        rem=[k for k in range(3) if k!=a]
        def line(v):
            ix=tuple(v if k==b else ALL for k in rem)
            return self.t1[(s,*ix)]
        if stage==0:
            self.ds[s]=self.term[ts,:,:,:,1-c].astype(bf)
        elif stage in (1,3):
            if stage==3:
                self.t1[s]=plane(xyz[a])+self.a2r[s,0].astype(f32)+self.a2r[s,1].astype(f32)
            axis,get,dst=(a,plane,self.a1s) if stage==1 else (b,line,self.b1s)
            dst[s]=get((xyz[axis]+2)%RING).astype(bf)
        elif stage in (2,RING):
            axis,get,dst,A,B,nd=(a,plane,self.a2s,self.a1A,self.a1B,2) if stage==2 else (b,line,self.b2s,self.b1A,self.b1B,1)
            lead=(ALL,)*nd
            p,q=(xyz[axis]+sigma+RING)%RING,(xyz[axis]-sigma+RING)%RING
            vp,vq=get(p),get(q)
            st=lambda k,r,cl,v: dst.__setitem__((s,k,*lead,r,cl),v.astype(bf))
            cut=lambda v,r,cl: v[(*lead,slice(r.start,r.start+r.size),slice(cl.start,cl.start+cl.size))]
            st(0,ra,ca,cut(vp,ra,ca)+A[s].astype(f32)); st(0,rb,cb,cut(vp,rb,cb))
            st(1,ra,ca,cut(vq,ra,ca)); st(1,rb,cb,cut(vq,rb,cb)+B[s].astype(f32))
        elif stage==5:
            self.t2[s]=line(xyz[b])+self.b2r[s,0].astype(f32)+self.b2r[s,1].astype(f32)
            for d in (1,2,3):
                self.cs[s,d-1]=self.t2[s,(xyz[cx]+d)%RING].astype(bf)
        else:
            v=self.t2[s,xyz[cx]]
            for d in range(3): v=v+self.cr[s,d].astype(f32)
            self.out(item,v.astype(bf))
        if stage<6:
            for cp in self.copies(stage,item): cp.start()

HC=((pl.ds(0,8),pl.ds(0,LANES)),(pl.ds(0,8),pl.ds(LANES,LANES)))
HR=((pl.ds(0,16),pl.ds(0,LANES)),(pl.ds(16,8),pl.ds(0,LANES)))

def rs_kernel(L,ng,nd,tg0,tg1,tu0,tu1,td0,td1,og,ou,od,odp,vg,vu,vd,lsem,*scr):
    n1=len(Scatter.scratch(8,COLS,HC))
    keys=list(Scatter.scratch(8,COLS,HC))
    pack=lambda k: dict(zip(keys,scr[k*n1:(k+1)*n1],strict=True))
    entry_barrier()
    items=L*ng
    lay=lambda i: L-1-i//ng
    idx=lambda i: lay(i)*ng+i%ng
    cols=lambda i: pl.ds(pl.multiple_of(i%ng*COLS,COLS),COLS)
    def outg(i,v): og[lay(i),:,cols(i)]=v
    def outu(i,v): ou[lay(i),:,cols(i)]=v
    def outd(k,v): odp[L-1-k//nd,:,pl.ds(pl.multiple_of(k%nd*LANES,LANES),LANES)]=v
    eg=Scatter(ORDERS[0],vg,outg,HC,pack(0))
    eu=Scatter(ORDERS[1],vu,outu,HC,pack(1))
    ed=Scatter(ORDERS[2],vd,outd,HR,pack(2))
    dk=lambda i: i//ng*nd+i%ng
    didx=lambda k: (L-1-k//nd)*nd+k%nd
    def load(m,i,go):
        v=(vg,vu,vd)[m]
        k,slot=(i%ng,i%RING) if m<2 else (i%ng,dk(i)%RING)
        for l,src in enumerate(((tg0,tg1),(tu0,tu1),(td0,td1))[m]):
            @pl.when(lay(i)==l)
            def _():
                cp=pltpu.make_async_copy(src.at[k],v.at[slot],lsem.at[m,i%2])
                cp.start() if go else cp.wait()
    def loads(i,go):
        load(0,i,go); load(1,i,go)
        @pl.when(i%ng<nd)
        def _(): load(2,i,go)
    loads(0,True)
    def tick(t,carry):
        for stage in reversed(range(7)):
            i=t-stage
            @pl.when((i>=0)&(i<items))
            def _():
                if stage==0: loads(i,False)
                eg.run(stage,i); eu.run(stage,i)
                @pl.when(i%ng<nd)
                def _(): ed.run(stage,dk(i))
        @pl.when(t+1<items)
        def _(): loads(t+1,True)
        return carry
    lax.fori_loop(0,items+6,tick,0)
    od[ALLOF]=odp[:,0:ROWS,:]

def reduce_scatter(tg,tu,td,L,F,D):
    ng,nd=F//COLS,D//LANES
    def flat(R,n,h): return list(Scatter.scratch(R,n,h).values())
    f=pl.pallas_call(functools.partial(rs_kernel,L,ng,nd),
        out_shape=[jax.ShapeDtypeStruct((L,8,F),bf)]*2+[jax.ShapeDtypeStruct((L,ROWS,D),bf)],
        in_specs=[pl.BlockSpec(memory_space=pl.ANY)]*6,
        out_specs=[pl.BlockSpec(memory_space=pltpu.VMEM)]*3,
        scratch_shapes=[pltpu.VMEM((L,PAD,D),bf),pltpu.VMEM((RING,RING,RING,RING,2,8,COLS),f32),pltpu.VMEM((RING,RING,RING,RING,2,8,COLS),f32),pltpu.VMEM((RING,RING,RING,RING,2,PAD,LANES),f32),
            pltpu.SemaphoreType.DMA((3,2))]+flat(8,COLS,HC)*2+flat(PAD,LANES,HR),
        compiler_params=pltpu.CompilerParams(collective_id=1,has_side_effects=True,vmem_limit_bytes=60<<20),name="scatter")
    return tuple(f(*tg,*tu,*td))

M,D,F=2048,1024,2816
NG=11
BM=COLS
def dot(a,b,ca=1,cb=0):
    return lax.dot_general(a,b,(((ca,),(cb,)),((),())),preferred_element_type=f32)
CP=lambda mb: pltpu.CompilerParams(vmem_limit_bytes=mb<<20)
S=jax.ShapeDtypeStruct
def normed(h):
    wide=h.astype(f32)
    return (wide*lax.rsqrt(jnp.mean(wide*wide,-1,keepdims=True)+1e-6)).astype(bf)
def cost(n): return pl.CostEstimate(flops=2*M*D*F*n,bytes_accessed=1<<PAD,transcendentals=0)

def norm_kernel(h_ref,a_ref,at_ref):
    a=normed(h_ref[ALLOF])
    a_ref[ALLOF]=a
    at_ref[ALLOF]=a.T
def norm(h):
    return pl.pallas_call(norm_kernel,grid=(M//BM,),in_specs=[pl.BlockSpec((BM,D),lambda i:(i,0))],
        out_specs=[pl.BlockSpec((BM,D),lambda i:(i,0)),pl.BlockSpec((D,BM),lambda i:(0,i))],
        out_shape=[S((M,D),bf),S((D,M),bf)],compiler_params=CP(32),name="norm")(h)

def gu_kernel(a_ref,wg_ref,wu_ref,g_ref,u_ref,pt_ref):
    for r in range(0,M,SUB):
        rows=pl.ds(r,SUB)
        g=dot(a_ref[rows,:],wg_ref[0])
        u=dot(a_ref[rows,:],wu_ref[0])
        s=jax.nn.sigmoid(g)
        b=g*s
        g_ref[0,rows,:]=u*(s+b*(1-s)); u_ref[0,rows,:]=b
        pt_ref[:,rows]=(b*u).astype(bf).T
def gate_up(l,a,wg,wu):
    return pl.pallas_call(gu_kernel,grid=(NG,),in_specs=[pl.BlockSpec((M,D),lambda j:(0,0)),pl.BlockSpec((1,D,COLS),lambda j:(l*NG+j,0,0)),pl.BlockSpec((1,D,COLS),lambda j:(l*NG+j,0,0))],
        out_specs=[pl.BlockSpec((1,M,COLS),lambda j:(j,0,0))]*2+[pl.BlockSpec((COLS,M),lambda j:(j,0))],
        out_shape=[S((NG,M,COLS),f32)]*2+[S((F,M),bf)],compiler_params=CP(60),cost_estimate=cost(2),name="gate_up")(a,wg,wu)

def compact_kernel(w_ref,o_ref):
    def group(k,c):
        v=w_ref[0,pl.ds(k*8,8)].astype(f32)
        o_ref[pl.ds(pl.multiple_of(k*GROUP,GROUP),GROUP),:]=jnp.concatenate([v[d,0:ROWS] for d in range(8)],0).astype(bf)
        return c
    lax.fori_loop(0,16,group,0)
def compact(w):
    n=w.shape[0]//2
    return [pl.pallas_call(compact_kernel,grid=(n,),in_specs=[pl.BlockSpec((1,LANES,PAD,LANES),lambda k:(l*n+k,0,0,0))],
        out_specs=pl.BlockSpec((F,LANES),lambda k:(0,k)),out_shape=S((F,D),bf),compiler_params=CP(32),name="compact")(w) for l in range(2)]

def down_kernel(pt_ref,w_ref,h_ref,h1_ref,a_ref,at_ref):
    y=dot(pt_ref[ALLOF],w_ref[ALLOF],0,0).astype(bf)
    h=h_ref[ALLOF]+y
    h1_ref[ALLOF]=h
    a=normed(h)
    a_ref[ALLOF]=a
    at_ref[ALLOF]=a.T
def down(pt,w,h):
    return pl.pallas_call(down_kernel,grid=(M//BM,),in_specs=[pl.BlockSpec((F,BM),lambda i:(0,i)),pl.BlockSpec((F,D),lambda i:(0,0)),pl.BlockSpec((BM,D),lambda i:(i,0))],
        out_specs=[pl.BlockSpec((BM,D),lambda i:(i,0))]*2+[pl.BlockSpec((D,BM),lambda i:(0,i))],
        out_shape=[S((M,D),bf)]*2+[S((D,M),bf)],compiler_params=CP(60),cost_estimate=cost(1),name="down")(pt,w,h)

def wd_kernel(pt_ref,dh_ref,t_ref,acc):
    acc[ALLOF]=dot(pt_ref[ALLOF],dh_ref[ALLOF])
    def group(k,c):
        for half in range(2):
            v=acc[pl.ds(pl.multiple_of(k*GROUP,GROUP),GROUP),pl.ds(half*LANES,LANES)]
            for d in range(8):
                t_ref[half,k*8+d,0:ROWS,:]=v[ROWS*d:ROWS*d+ROWS]
        return c
    lax.fori_loop(0,16,group,0)
def grad_down(pt,dh):
    return pl.pallas_call(wd_kernel,grid=(D//COLS,),in_specs=[pl.BlockSpec((F,M),lambda n:(0,0)),pl.BlockSpec((M,COLS),lambda n:(0,n))],
        out_specs=pl.BlockSpec((2,LANES,PAD,LANES),lambda n:(n,0,0,0)),out_shape=S((8,LANES,PAD,LANES),f32),
        scratch_shapes=[pltpu.VMEM((F,COLS),f32)],compiler_params=CP(60),cost_estimate=cost(1),name="grad_down")(pt,dh)

def b1_kernel(dh_ref,wd_ref,g_ref,u_ref,at_ref,dg_ref,du_ref,tg_ref,tu_ref,dgs,dus):
    j=pl.program_id(0)
    def front():
        for r in range(0,M,SUB):
            rows=pl.ds(r,SUB)
            dp=dot(dh_ref[rows,:],wd_ref[ALLOF],1,1).astype(bf).astype(f32)
            dg=(dp*g_ref[0,rows,:]).astype(bf)
            du=(dp*u_ref[0,rows,:]).astype(bf)
            dg_ref[0,rows,:]=dg; du_ref[0,rows,:]=du
            dgs[j%2,rows,:]=dg; dus[j%2,rows,:]=du
    def back():
        tg_ref[0]=dot(at_ref[ALLOF],dgs[(j+1)%2])
        tu_ref[0]=dot(at_ref[ALLOF],dus[(j+1)%2])
    @pl.when(j==0)
    def _(): front()
    @pl.when((j>0)&(j<NG))
    def _():
        front(); back()
    @pl.when(j==NG)
    def _(): back()
def grad_gate_up(dh,wd,g,u,at):
    here=lambda j: jnp.minimum(j,NG-1)
    last=lambda j: jnp.maximum(j-1,0)
    blk=pl.BlockSpec((1,M,COLS),lambda j:(here(j),0,0))
    return pl.pallas_call(b1_kernel,grid=(NG+1,),in_specs=[pl.BlockSpec((M,D),lambda j:(0,0)),pl.BlockSpec((COLS,D),lambda j:(here(j),0)),blk,blk,pl.BlockSpec((D,M),lambda j:(0,0))],
        out_specs=[blk]*2+[pl.BlockSpec((1,D,COLS),lambda j:(last(j),0,0))]*2,
        out_shape=[S((NG,M,COLS),bf)]*2+[S((NG,D,COLS),f32)]*2,scratch_shapes=[pltpu.VMEM((2,M,COLS),bf)]*2,
        compiler_params=CP(60),cost_estimate=cost(3),name="grad_gate_up")(dh,wd,g,u,at)

def b2_kernel(dg_ref,du_ref,wg_ref,wu_ref,h_ref,dh_ref,o_ref):
    acc=dot(dg_ref[0],wg_ref[0],1,1)+dot(du_ref[0],wu_ref[0],1,1)
    for j in range(1,NG):
        acc+=dot(dg_ref[j],wg_ref[j],1,1)
        acc+=dot(du_ref[j],wu_ref[j],1,1)
    d=acc.astype(bf).astype(f32)
    h=h_ref[ALLOF].astype(f32)
    scale=lax.rsqrt(jnp.mean(h*h,-1,keepdims=True)+1e-6)
    t=jnp.sum(d*h,-1,keepdims=True)*(scale*scale*scale)*(1.0/D)
    o_ref[ALLOF]=dh_ref[ALLOF]+(d*scale-h*t).astype(bf)
def grad_h(l,dg,du,wg,wu,h,dh):
    row=pl.BlockSpec((BM,D),lambda i:(i,0))
    blk=pl.BlockSpec((NG,BM,COLS),lambda i:(0,i,0))
    w=pl.BlockSpec((NG,D,COLS),lambda i:(l,0,0),pipeline_mode=pl.Buffered(1))
    return pl.pallas_call(b2_kernel,grid=(M//BM,),in_specs=[blk,blk,w,w,row,row],out_specs=row,out_shape=S((M,D),bf),
        compiler_params=CP(60),cost_estimate=cost(2),name="grad_h")(dg,du,wg,wu,h,dh)


def step(x,dy,wg,wu,wd):
    x,dy=x[0],dy[0]
    gg,gu,gd=gather(wg,wu,wd)
    gg,gu=(t.reshape(2*NG,D,COLS) for t in (gg,gu))
    down_w=compact(gd.reshape(16,LANES,PAD,LANES))
    a0,at0=norm(x)
    g0,u0,pt0=gate_up(0,a0,gg,gu)
    h1,a1,at1=down(pt0,down_w[0],x)
    g1,u1,pt1=gate_up(1,a1,gg,gu)
    dh=dy
    terms=[None,None]
    for l,(g,u,pt,at,h) in ((1,(g1,u1,pt1,at1,h1)),(0,(g0,u0,pt0,at0,x))):
        td=grad_down(pt,dh)
        dg,du,tg,tu=grad_gate_up(dh,down_w[l],g,u,at)
        terms[l]=(tg.reshape(NG,RING,RING,RING,2,8,COLS),tu.reshape(NG,RING,RING,RING,2,8,COLS),td.reshape(8,RING,RING,RING,2,PAD,LANES))
        dh=grad_h(l,dg,du,gg,gu,h,dh)
    og,ou,od=reduce_scatter(*zip(*terms,strict=True),2,F,D)
    return dh[None],og,ou,od

def solution(mesh):
    tok=P(("rep","dp"),None,None)
    w=P(None,"dp",None)
    o=P("rep","dp",None)
    return jax.shard_map(step,mesh=mesh,in_specs=(tok,tok,w,w,w),out_specs=(tok,o,o,o),check_vma=False)
```

time: 3090 us -> 615 us (0.20)
  waiting for transfers between devices: 2170 us -> 0 us
  Pallas kernels: 0 us -> 592 us
  blocking collectives: 368 us -> 0 us
  matrix products: 344 us -> 0 us
  other arithmetic: 80.2 us -> 0 us
  starting transfers between devices: 69.3 us -> 0 us
    unnamed x36 -> x0, waiting for transfers between devices: 1910 us -> none
    pallas_call x0 -> x14, Pallas kernels: none -> 592 us  [the longest x1 152 us: gather(): return tuple(f(wg, wu, wd))]
    unnamed x1 -> x0, blocking collectives: 368 us -> none
    dot_general x17 -> x0, matrix products: 344 us -> none  [the longest x6 126 us: layer(): up = jnp.dot(a, w['w_up'], preferred_element_type=jnp.float32)]
    squeeze x6 -> x0, waiting for transfers between devices: 259 us -> none  [stack(): h = layer(h, {name: w[number] for name, w in weights.items()})]
    unnamed x26 -> x0, starting transfers between devices: 69 us -> none
    unnamed x5 -> x0, other arithmetic: 62.9 us -> none
  transfers between devices with their start and end apart: 32 -> 0, of which waited for: 9 -> 0; matrix products, arithmetic and copies ran while one was open for 27% -> 0% of each run, Pallas kernels for 0% -> 0%
where the time goes in v1:
time: 615 us
  Pallas kernels  592 us (96%)
  local copies, waits for them, and re-layouts  21.9 us (4%)
    pallas_call x1, Pallas kernels, gather(): return tuple(f(wg, wu, wd))  152 us
    pallas_call x1, Pallas kernels, reduce_scatter(): return tuple(f(*tg, *tu, *td))  141 us
    pallas_call x2, Pallas kernels, grad_gate_up(): pl.pallas_call(b1_kernel, grid=(NG + 1,), in_specs=[pl.BlockSpec((M, D),...  98.2 us
    pallas_call x2, Pallas kernels, grad_h(): pl.pallas_call(b2_kernel, grid=(M // BM,), in_specs=[blk, blk, w, w, row,...  66.5 us
    pallas_call x2, Pallas kernels, gate_up(): pl.pallas_call(gu_kernel, grid=(NG,), in_specs=[pl.BlockSpec((M, D), lamb...  63.8 us
    pallas_call x2, Pallas kernels, grad_down(): pl.pallas_call(wd_kernel, grid=(D // COLS,), in_specs=[pl.BlockSpec((F, M...  40.4 us
    unnamed x16, local copies, waits for them, and re-layouts  21.9 us
    pallas_call x1, Pallas kernels, down(): pl.pallas_call(down_kernel, grid=(M // BM,), in_specs=[pl.BlockSpec((F, B...  20.4 us

profile of v1, /device:TPU:0, one launch (start us, length us, event | category | flops | bytes accessed | tf_op | source)
XLA Modules:
  0.0 614.9 jit_solution(17879207404939551444)
XLA Ops:
  0.6 1.6 copy.9.wd
  2.2 0.0 copy-start.3
  2.2 2.2 copy-done.3
  4.4 3.0 norm.1
  7.4 0.0 copy-start.4
  7.4 2.0 copy-done.4
  9.4 0.0 copy-start.5
  9.4 2.0 copy-done.5
  11.4 152.2 %gather.1 = (bf16[22,4,4,4,2,8,256]{6,5,4,3,2,1,0:T(8,128)(2,1)}, bf16[22,4,4,4,2,8,256]{6,5,4,3,2,1,0:T(8,128)(2,1)}, bf16[16,4,4,4,2,24,128]{6,5,4,3,2,1,0:T(8,128)(2,1)}) custom-call(bf16[2,8,2816]{2,1,0:T(8,128)(2,1)} %wg.1, bf16[2,8,2816]{2,1,0:T(8,128)(2,1)} %wu.1, bf16[2,22,1024]{2,1,0:T(8,128)(2,1)} %copy.9.wd), custom_call_target="tpu_custom_call" | custom-call | tf_op jit(solution)/shard_map/gather/pallas_call | solution.py:133
  163.6 0.0 copy-start
  163.6 4.6 copy-done
  168.2 3.5 compact.3.w_ref.wd_ref
  171.7 0.0 copy-start.1
  171.7 2.4 copy-done.1
  174.2 3.5 compact.2.wd_ref
  177.7 0.0 copy-start.2
  177.8 2.4 copy-done.2
  180.2 31.9 %gate_up.2 = (f32[11,2048,256]{2,1,0:T(8,128)}, f32[11,2048,256]{2,1,0:T(8,128)}, bf16[2816,2048]{1,0:T(8,128)(2,1)}) custom-call(bf16[2048,1024]{1,0:T(8,128)(2,1)} %copy-done.5, bf16[22,1024,256]{2,1,0:T(8,128)(2,1)} %bitcast.23, bf16[22,1024,256]{2,1,0:T(8,128)(2,1)} %bitcast.27), custom_call_target="tpu_custom_call" | custom-call | flops 23622320128 | bytes 16777216 | tf_op jit(solution)/shard_map/gate_up/pallas_call | solution.py:311
  212.1 20.4 %down.1 = (bf16[2048,1024]{1,0:T(8,128)(2,1)}, bf16[2048,1024]{1,0:T(8,128)(2,1)}, bf16[1024,2048]{1,0:T(8,128)(2,1)}) custom-call(bf16[2816,2048]{1,0:T(8,128)(2,1)} %get-tuple-element.33.pt_ref, bf16[2816,1024]{1,0:T(8,128)(2,1)} %copy-done.1, bf16[2048,1024]{1,0:T(8,128)(2,1)} %bitcast.14), custom_call_target="tpu_custom_call" | custom-call | flops 11811160064 | bytes 16777216 | tf_op jit(solution)/shard_map/down/pallas_call | solution.py:334
  232.5 31.9 %gate_up.3 = (f32[11,2048,256]{2,1,0:T(8,128)}, f32[11,2048,256]{2,1,0:T(8,128)}, bf16[2816,2048]{1,0:T(8,128)(2,1)}) custom-call(bf16[2048,1024]{1,0:T(8,128)(2,1)} %get-tuple-element.34.a_ref, bf16[22,1024,256]{2,1,0:T(8,128)(2,1)} %bitcast.24, bf16[22,1024,256]{2,1,0:T(8,128)(2,1)} %bitcast.28), custom_call_target="tpu_custom_call" | custom-call | flops 23622320128 | bytes 16777216 | tf_op jit(solution)/shard_map/gate_up/pallas_call | solution.py:311
  264.4 49.0 %grad_gate_up.2 = (bf16[11,2048,256]{2,1,0:T(8,128)(2,1)}, bf16[11,2048,256]{2,1,0:T(8,128)(2,1)}, f32[11,1024,256]{2,1,0:T(8,128)}, f32[11,1024,256]{2,1,0:T(8,128)}) custom-call(bf16[2048,1024]{1,0:T(8,128)(2,1)} %bitcast.31, bf16[2816,1024]{1,0:T(8,128)(2,1)} %copy-done.2, f32[11,2048,256]{2,1,0:T(8,128)} %get-tuple-element.35.g_ref, ...), custom_call_target="tpu_custom_call" | custom-call | flops 35433480192 | bytes 16777216 | tf_op jit(solution)/shard_map/grad_gate_up/pallas_call | solution.py:376
  313.4 33.3 %grad_h.2.dh_ref = bf16[2048,1024]{1,0:T(8,128)(2,1)} custom-call(bf16[11,2048,256]{2,1,0:T(8,128)(2,1)} %get-tuple-element.38.dg_ref, bf16[11,2048,256]{2,1,0:T(8,128)(2,1)} %get-tuple-element.39.du_ref, bf16[22,1024,256]{2,1,0:T(8,128)(2,1)} %bitcast.25, bf16[22,1024,256]{2,1,0:T(8,128)(2,1)} %bitcast.29, bf16[2048,1024]{1,0:T(8,128)(2,1)} %get-tuple-element.40.h_ref, ...), custom_call_target="tpu_custom_call" | custom-call | flops 23622320128 | bytes 16777216 | tf_op jit(solution)/shard_map/grad_h/pallas_call | solution.py:395
  346.7 49.2 %grad_gate_up.3 = (bf16[11,2048,256]{2,1,0:T(8,128)(2,1)}, bf16[11,2048,256]{2,1,0:T(8,128)(2,1)}, f32[11,1024,256]{2,1,0:T(8,128)}, f32[11,1024,256]{2,1,0:T(8,128)}) custom-call(bf16[2048,1024]{1,0:T(8,128)(2,1)} %grad_h.2.dh_ref, bf16[2816,1024]{1,0:T(8,128)(2,1)} %copy-done.1, f32[11,2048,256]{2,1,0:T(8,128)} %get-tuple-element.41.g_ref, ...), custom_call_target="tpu_custom_call" | custom-call | flops 35433480192 | bytes 16777216 | tf_op jit(solution)/shard_map/grad_gate_up/pallas_call | solution.py:376
  395.8 33.2 %grad_h.3 = bf16[2048,1024]{1,0:T(8,128)(2,1)} custom-call(bf16[11,2048,256]{2,1,0:T(8,128)(2,1)} %get-tuple-element.44.dg_ref, bf16[11,2048,256]{2,1,0:T(8,128)(2,1)} %get-tuple-element.45.du_ref, bf16[22,1024,256]{2,1,0:T(8,128)(2,1)} %bitcast.26, bf16[22,1024,256]{2,1,0:T(8,128)(2,1)} %bitcast.30, bf16[2048,1024]{1,0:T(8,128)(2,1)} %bitcast.15, ...), custom_call_target="tpu_custom_call" | custom-call | flops 23622320128 | bytes 16777216 | tf_op jit(solution)/shard_map/grad_h/pallas_call | solution.py:395
  429.1 20.2 %grad_down.2 = f32[8,128,24,128]{3,2,1,0:T(8,128)} custom-call(bf16[2816,2048]{1,0:T(8,128)(2,1)} %get-tuple-element.33.pt_ref, bf16[2048,1024]{1,0:T(8,128)(2,1)} %grad_h.2.dh_ref), custom_call_target="tpu_custom_call" | custom-call | flops 11811160064 | bytes 16777216 | tf_op jit(solution)/shard_map/grad_down/pallas_call | solution.py:348
  449.3 20.2 %grad_down.3 = f32[8,128,24,128]{3,2,1,0:T(8,128)} custom-call(bf16[2816,2048]{1,0:T(8,128)(2,1)} %get-tuple-element.50.pt_ref, bf16[2048,1024]{1,0:T(8,128)(2,1)} %bitcast.33), custom_call_target="tpu_custom_call" | custom-call | flops 11811160064 | bytes 16777216 | tf_op jit(solution)/shard_map/grad_down/pallas_call | solution.py:348
  469.5 140.7 %scatter.1 = (bf16[2,8,2816]{2,1,0:T(8,128)(2,1)}, bf16[2,8,2816]{2,1,0:T(8,128)(2,1)}, bf16[2,22,1024]{2,1,0:T(8,128)(2,1)}) custom-call(f32[11,4,4,4,2,8,256]{6,5,4,3,2,1,0:T(8,128)} %bitcast.21, f32[11,4,4,4,2,8,256]{6,5,4,3,2,1,0:T(8,128)} %bitcast.19, f32[11,4,4,4,2,8,256]{6,5,4,3,2,1,0:T(8,128)} %bitcast.22, f32[11,4,4,4,2,8,256]{6,5,4,3,2,1,0:T(8,128)} %bitcast.20, ...), custom_call_target="tpu_custom_call" | custom-call | tf_op jit(solution)/shard_map/scatter/pallas_call | solution.py:278
  610.2 1.6 copy.10
  611.8 1.5 copy.13
  613.4 1.5 copy.14
Async XLA Ops:
  2.2 2.2 copy-start.3
  7.4 2.0 copy-start.4
  9.4 2.0 copy-start.5
  163.6 4.6 copy-start
  171.7 2.5 copy-start.1
  177.7 2.4 copy-start.2

commit v2 on v1

--- a/solution.py
+++ b/solution.py
@@ -7,82 +7,115 @@
 from jax.experimental.pallas import tpu as pltpu
 from jax.sharding import PartitionSpec as P
 
+MESH=pl.DeviceIdType.MESH
 bf=jnp.bfloat16
-RING=4
-COLS=256
-LANES=128
-ROWS=22
-PAD=24
-GROUP=8*ROWS
+f32=jnp.float32
+S=jax.ShapeDtypeStruct
 ALLOF=...
-f32=jnp.float32
-SUB=COLS
-MESH=pl.DeviceIdType.MESH
-W=8
+ALL=slice(None)
+M,D,F,L=2048,1024,2816,2
+RING,COLS,LANES=4,256,128
+CHIPS=(RING,)*3
+TORUS=(*CHIPS,2)
+R8,ROWS,PAD,EIGHT=8,22,24,8
+GROUP=EIGHT*ROWS
+NG,ND=F//COLS,D//LANES
+ITEMS=L*NG
+BM=256
+TILES=M//BM
 ORDERS=((2,1,0),(0,2,1),(1,0,2))
+HALF_COLS=((pl.ds(0,R8),pl.ds(0,LANES)),(pl.ds(0,R8),pl.ds(LANES,LANES)))
+HALF_ROWS=((pl.ds(0,16),pl.ds(0,LANES)),(pl.ds(16,8),pl.ds(0,LANES)))
+DMA=pltpu.SemaphoreType.DMA
+ANY=pl.BlockSpec(memory_space=pl.ANY)
+INVMEM=pl.BlockSpec(memory_space=pltpu.VMEM)
+VMEM=pltpu.VMEM
+
+def dot(a,b,ca=1,cb=0):
+    return lax.dot_general(a,b,(((ca,),(cb,)),((),())),preferred_element_type=f32)
+
+def rms(h):
+    return lax.rsqrt(jnp.mean(h*h,-1,keepdims=True)+1e-6)
+
+def normed(h):
+    wide=h.astype(f32)
+    return (wide*rms(wide)).astype(bf)
+
+def aligned(i,n):
+    return pl.ds(pl.multiple_of(i*n,n),n)
+
+def params(n,mb):
+    return pltpu.CompilerParams(collective_id=n,has_side_effects=True,vmem_limit_bytes=mb<<20)
+
 
 def coords():
     me=lax.axis_index("dp")
-    return (me//32, (me//8)%RING, (me//2)%RING), me%2
+    chip=me//2
+    return (chip//RING//RING,chip//RING%RING,chip%RING),me%2
 
 def dev(xyz,c):
-    return {"dp": ((xyz[0]*RING+xyz[1])*RING+xyz[2])*2+c}
+    return {"dp":((xyz[0]*RING+xyz[1])*RING+xyz[2])*2+c}
 
 def moved(xyz,axis,to):
     return tuple(to if k==axis else v for k,v in enumerate(xyz))
 
-def region(g,item,full,xyz,c,rows=slice(None),cols=slice(None)):
-    ix=tuple(slice(None) if k in full else xyz[k] for k in range(3))
-    return g.at[(item,*ix,c,rows,cols)]
+def at(axis,v,axes=(0,1,2)):
+    return tuple(v if k==axis else ALL for k in axes)
+
+def sides(xyz,axis,c):
+    sigma=1-2*c
+    return (xyz[axis]+sigma+RING)%RING,(xyz[axis]-sigma+RING)%RING
+
+def others(xyz,axis):
+    return [moved(xyz,axis,(xyz[axis]+d)%RING) for d in range(1,RING)]
+
+def remote(src,dst,sems,slot,k,xyz,c):
+    send,recv=sems
+    return pltpu.make_async_remote_copy(src_ref=src,dst_ref=dst,send_sem=send.at[slot,k],recv_sem=recv.at[slot,k],
+        device_id=dev(xyz,c),device_id_type=MESH)
 
 def entry_barrier():
     xyz,c=coords()
     b=pltpu.get_barrier_semaphore()
-    n=0
-    for axis in range(3):
-        for d in (1,2,3):
-            pl.semaphore_signal(b,inc=1,device_id=dev(moved(xyz,axis,(xyz[axis]+d)%RING),c),device_id_type=MESH)
-            n+=1
-    pl.semaphore_signal(b,inc=1,device_id=dev(xyz,1-c),device_id_type=MESH)
-    pl.semaphore_wait(b,n+1)
+    reach=[(to,c) for axis in range(3) for to in others(xyz,axis)]+[(xyz,1-c)]
+    for to in reach:
+        pl.semaphore_signal(b,inc=1,device_id=dev(*to),device_id_type=MESH)
+    pl.semaphore_wait(b,len(reach))
+
+
+SLOTS=4
+G_OFF=(0,2,4,6,8,10,11)
+G_DEPTH=G_OFF[-1]
+DOWN_STEPS=TILES
+F_STEPS=ITEMS+DOWN_STEPS
 
 class Gather:
-    STAGES=7
-    def __init__(self,order,g,own,send,recv,local,halves):
-        self.order,self.g,self.own,self.send,self.recv,self.local,self.halves=order,g,own,send,recv,local,halves
+    def __init__(self,order,g,own,halves,sems,local):
+        self.order,self.g,self.own,self.halves,self.sems,self.local=order,g,own,halves,sems,local
+    def region(self,item,full,xyz,c,part=(ALL,ALL)):
+        return self.g.at[(item,*(ALL if k in full else xyz[k] for k in range(3)),c,*part)]
     def copies(self,stage,item):
         xyz,c=coords()
         a,b,last=self.order
-        g=self.g
-        slot=item%W
-        sigma=1-2*c
-        def copy(k,src,dst,to,tc=None):
-            return pltpu.make_async_remote_copy(src_ref=src,dst_ref=dst,send_sem=self.send.at[slot,k],recv_sem=self.recv.at[slot,k],
-                device_id=dev(to,c if tc is None else tc),device_id_type=MESH)
+        def copy(k,src,dst,to,tc=c):
+            return remote(src,dst,self.sems,item%SLOTS,k,to,tc)
         if stage==0:
-            mine=region(g,item,(),xyz,c)
-            out=[copy(d-1,self.own(item),mine,moved(xyz,a,(xyz[a]+d)%RING)) for d in (1,2,3)]
-            return out
-        if stage in (1,3):
-            axis,full=(b,(a,)) if stage==1 else (last,(a,b))
-            r=region(g,item,full,xyz,c)
-            k=3 if stage==1 else 7
-            p,q=(xyz[axis]+sigma+RING)%RING,(xyz[axis]-sigma+RING)%RING
-            return [copy(k,r,r,moved(xyz,axis,p)),copy(k+1,r,r,moved(xyz,axis,q))]
-        if stage in (2,RING):
-            axis,full=(b,(a,)) if stage==2 else (last,(a,b))
-            k=5 if stage==2 else 9
-            p,q=(xyz[axis]+sigma+RING)%RING,(xyz[axis]-sigma+RING)%RING
-            (ra,ca),(rb,cb)=self.halves
-            fromq=region(g,item,full,moved(xyz,axis,q),c,ra,ca)
-            fromp=region(g,item,full,moved(xyz,axis,p),c,rb,cb)
-            return [copy(k,fromq,fromq,moved(xyz,axis,p)),copy(k+1,fromp,fromp,moved(xyz,axis,q))]
+            mine=self.region(item,(),xyz,c)
+            return [copy(k,self.own(item),mine,to) for k,to in enumerate(others(xyz,a))]
         if stage==5:
-            r=region(g,item,(0,1,2),xyz,c)
-            return [copy(11,r,r,xyz,1-c)]
+            mine=self.region(item,(0,1,2),xyz,c)
+            return [copy(11,mine,mine,xyz,1-c)]
+        axis,full,k=(b,(a,),3) if stage<3 else (last,(a,b),7)
+        p,q=sides(xyz,axis,c)
+        if stage%2:
+            mine=self.region(item,full,xyz,c)
+            return [copy(k,mine,mine,moved(xyz,axis,p)),copy(k+1,mine,mine,moved(xyz,axis,q))]
+        fromq=self.region(item,full,moved(xyz,axis,q),c,self.halves[0])
+        fromp=self.region(item,full,moved(xyz,axis,p),c,self.halves[1])
+        return [copy(k+2,fromq,fromq,moved(xyz,axis,p)),copy(k+3,fromp,fromp,moved(xyz,axis,q))]
     def own_copy(self,item):
         xyz,c=coords()
-        return pltpu.make_async_copy(self.own(item),region(self.g,item,(),xyz,c),self.local.at[item%W])
+        return pltpu.make_async_copy(self.own(item),self.region(item,(),xyz,c),self.local.at[item%SLOTS])
     def run(self,stage,item):
         if stage>0:
             for cp in self.copies(stage-1,item): cp.wait()
@@ -91,48 +124,132 @@
             for cp in self.copies(stage,item): cp.start()
             if stage==0: self.own_copy(item).start()
 
-def ag_kernel(items,counts,wg,wu,wd,gg,gu,gd,wdp,*sems):
-    L=wd.shape[0]
-    wdp[ALLOF]=jnp.zeros_like(wdp)
+def f_kernel(x,wg,wu,wd,gg,gu,gd,ga,gb,pt,at_,h1,wc,
+        wdp,xv,av,ptv,wcv,wv,dv,abv,atv,hv,xsem,wsem,dsem,absem,ptsem,atsem,hsem,wcsem,*gsems):
     for l in range(L):
         wdp[l,0:ROWS,:]=wd[l]
+        wdp[l,ROWS:PAD,:]=jnp.zeros((PAD-ROWS,D),bf)
+    load_x=pltpu.make_async_copy(x,xv,xsem)
+    load_x.start()
     entry_barrier()
-    ng,nd=counts
-    half_c=((slice(None),pl.ds(0,LANES)),(slice(None),pl.ds(LANES,LANES)))
-    half_r=((pl.ds(0,16),slice(None)),(pl.ds(16,8),slice(None)))
-    own_g=lambda i: wg.at[i//ng,:,pl.ds(pl.multiple_of(i%ng*COLS,COLS),COLS)]
-    own_u=lambda i: wu.at[i//ng,:,pl.ds(pl.multiple_of(i%ng*COLS,COLS),COLS)]
-    own_d=lambda i: wdp.at[i//nd,:,pl.ds(pl.multiple_of(i%nd*LANES,LANES),LANES)]
-    eg=Gather(ORDERS[0],gg,own_g,*sems[0:3],half_c)
-    eu=Gather(ORDERS[1],gu,own_u,*sems[3:6],half_c)
-    ed=Gather(ORDERS[2],gd,own_d,*sems[6:9],half_r)
-    def tick(t,carry):
+    own_g=lambda i: wg.at[i//NG,:,aligned(i%NG,COLS)]
+    own_u=lambda i: wu.at[i//NG,:,aligned(i%NG,COLS)]
+    own_d=lambda k: wdp.at[k//ND,:,aligned(k%ND,LANES)]
+    eg=Gather(ORDERS[0],gg,own_g,HALF_COLS,gsems[0:2],gsems[2])
+    eu=Gather(ORDERS[1],gu,own_u,HALF_COLS,gsems[3:5],gsems[5])
+    ed=Gather(ORDERS[2],gd,own_d,HALF_ROWS,gsems[6:8],gsems[8])
+    down_of=lambda i: i//NG*ND+i%NG
+    def load_d(k):
+        return pltpu.make_async_copy(gd.at[k],dv.at[k%2],dsem.at[k%2])
+    def store_wc(l):
+        return pltpu.make_async_copy(wcv.at[l],wc.at[l],wcsem.at[l])
+    def compact(k):
+        load_d(k).wait()
+        def group(j,carry):
+            v=dv[k%2,j//RING,j%RING].reshape(EIGHT,PAD,LANES).astype(f32)
+            wcv[k//ND,aligned(j,GROUP),aligned(k%ND,LANES)]=jnp.concatenate([v[d,0:ROWS] for d in range(EIGHT)],0).astype(bf)
+            return carry
+        lax.fori_loop(0,16,group,0)
+        @pl.when(k%ND==ND-1)
+        def _(): store_wc(k//ND).start()
+    def tick(t):
+        i=t-G_DEPTH-1
+        @pl.when((i>=0)&(i<ITEMS)&(i%NG<ND))
+        def _(): compact(down_of(i))
         for stage in reversed(range(7)):
-            i=t-stage
-            @pl.when((i>=0)&(i<items))
+            i=t-G_OFF[stage]
+            @pl.when((i>=0)&(i<ITEMS))
             def _():
                 eg.run(stage,i); eu.run(stage,i)
-                @pl.when(i%ng<nd)
+                @pl.when(i%NG<ND)
                 def _():
-                    ed.run(stage,i//ng*nd+i%ng)
+                    ed.run(stage,down_of(i))
+                    if stage==6: load_d(down_of(i)).start()
+    item_of=lambda k: jnp.where(k<NG,k,k-DOWN_STEPS)
+    is_item=lambda k: ((k>=0)&(k<NG))|((k>=NG+DOWN_STEPS)&(k<F_STEPS))
+    def load_w(i):
+        return [pltpu.make_async_copy(g.at[i],wv.at[m,i%2],wsem.at[m,i%2]) for m,g in enumerate((gg,gu))]
+    def store_ab(i):
+        s=i%2
+        return [pltpu.make_async_copy(abv.at[m,s],o.at[i//NG,i%NG],absem.at[m,s]) for m,o in enumerate((ga,gb))]+[
+            pltpu.make_async_copy(ptv.at[aligned(i%NG,COLS)],pt.at[i//NG,aligned(i%NG,COLS)],ptsem.at[s])]
+    def store_at(l,r):
+        return pltpu.make_async_copy(atv.at[r%2],at_.at[l,:,aligned(r,BM)],atsem.at[r%2])
+    def store_h(r):
+        return pltpu.make_async_copy(hv.at[r%2],h1.at[aligned(r,BM)],hsem.at[r%2])
+    def put_a(l,r,h):
+        a=normed(h)
+        av[aligned(r,BM),:]=a
+        @pl.when(r>=2)
+        def _(): store_at(l,r-2).wait()
+        atv[r%2]=a.T
+        store_at(l,r).start()
+    def gate_up(i):
+        for cp in load_w(i): cp.wait()
+        @pl.when(i>=2)
+        def _():
+            for cp in store_ab(i-2): cp.wait()
+        s=i%2
+        w_gate,w_up=(wv[m,s].reshape(D,COLS) for m in range(2))
+        for r in range(TILES):
+            rows=pl.ds(r*BM,BM)
+            g=dot(av[rows,:],w_gate)
+            u=dot(av[rows,:],w_up)
+            sg=jax.nn.sigmoid(g)
+            b=g*sg
+            abv[0,s,rows,:]=u*(sg+b*(1-sg))
+            abv[1,s,rows,:]=b
+            ptv[aligned(i%NG,COLS),rows]=(b*u).astype(bf).T
+        for cp in store_ab(i): cp.start()
+    def down(r):
+        y=dot(ptv[:,aligned(r,BM)],wcv[0],0,0).astype(bf)
+        h=xv[aligned(r,BM),:]+y
+        @pl.when(r>=2)
+        def _(): store_h(r-2).wait()
+        hv[r%2]=h
+        store_h(r).start()
+        put_a(1,r,h)
+    tick(0)
+    load_x.wait()
+    def norm(r,carry):
+        put_a(0,r,xv[aligned(r,BM),:])
         return carry
-    lax.fori_loop(0,items+6,tick,0)
-
-def gather(wg,wu,wd):
-    L,_,F=wg.shape; D=wd.shape[2]
-    ng,nd=F//COLS,D//LANES
-    assert nd<=ng or L==1
-    items=L*ng
-    sem=pltpu.SemaphoreType.DMA
-    f=pl.pallas_call(functools.partial(ag_kernel,items,(ng,nd)),
-        out_shape=[jax.ShapeDtypeStruct((L*ng,RING,RING,RING,2,8,COLS),bf)]*2+[jax.ShapeDtypeStruct((L*nd,RING,RING,RING,2,PAD,LANES),bf)],
-        in_specs=[pl.BlockSpec(memory_space=pltpu.VMEM)]*3,
-        out_specs=[pl.BlockSpec(memory_space=pl.ANY)]*3,
-        scratch_shapes=[pltpu.VMEM((L,PAD,D),bf)]+[sem((W,12)),sem((W,12)),sem((W,))]*3,
-        compiler_params=pltpu.CompilerParams(collective_id=0,has_side_effects=True),name="gather")
-    return tuple(f(wg,wu,wd))
-
-ALL=slice(None)
+    lax.fori_loop(0,TILES,norm,0)
+    for r in (TILES-2,TILES-1): store_at(0,r).wait()
+    def step(t,carry):
+        k=t-G_DEPTH-1
+        tick(t)
+        @pl.when(is_item(k+1))
+        def _():
+            for cp in load_w(item_of(k+1)): cp.start()
+        @pl.when(is_item(k))
+        def _(): gate_up(item_of(k))
+        @pl.when((k>=NG)&(k<NG+DOWN_STEPS))
+        def _(): down(k-NG)
+        return carry
+    lax.fori_loop(1,F_STEPS+G_DEPTH+1,step,0)
+    for r in (TILES-2,TILES-1):
+        store_at(1,r).wait()
+        store_h(r).wait()
+    for i in (ITEMS-2,ITEMS-1):
+        for cp in store_ab(i): cp.wait()
+    for l in range(L): store_wc(l).wait()
+
+def forward(x,wg,wu,wd):
+    return pl.pallas_call(f_kernel,
+        out_shape=[S((ITEMS,*TORUS,R8,COLS),bf)]*2+[S((L*ND,*TORUS,PAD,LANES),bf)]+[S((L,NG,M,COLS),f32)]*2+[
+            S((L,F,M),bf),S((L,D,M),bf),S((M,D),bf),S((L,F,D),bf)],
+        in_specs=[ANY]+[INVMEM]*3,out_specs=[ANY]*9,
+        scratch_shapes=[VMEM((L,PAD,D),bf),VMEM((M,D),bf),VMEM((M,D),bf),VMEM((F,M),bf),VMEM((L,F,D),bf),VMEM((2,2,*TORUS,R8,COLS),bf),
+            VMEM((2,*TORUS,PAD,LANES),bf),VMEM((2,2,M,COLS),f32),VMEM((2,D,BM),bf),VMEM((2,BM,D),bf),
+            DMA,DMA((2,2)),DMA((2,)),DMA((2,2)),DMA((2,)),DMA((2,)),DMA((2,)),DMA((L,))]+[DMA((SLOTS,12)),DMA((SLOTS,12)),DMA((SLOTS,))]*3,
+        compiler_params=params(0,62),name="forward")(x,wg,wu,wd)
+
+HC=HALF_COLS
+HR=HALF_ROWS
+CP=lambda mb: pltpu.CompilerParams(vmem_limit_bytes=mb<<20)
+def cost(n): return pl.CostEstimate(flops=2*M*D*F*n,bytes_accessed=1<<24,transcendentals=0)
+SUB=256
 class Scatter:
     STAGES=7
     TW=RING
@@ -277,64 +394,6 @@
         compiler_params=pltpu.CompilerParams(collective_id=1,has_side_effects=True,vmem_limit_bytes=60<<20),name="scatter")
     return tuple(f(*tg,*tu,*td))
 
-M,D,F=2048,1024,2816
-NG=11
-BM=COLS
-def dot(a,b,ca=1,cb=0):
-    return lax.dot_general(a,b,(((ca,),(cb,)),((),())),preferred_element_type=f32)
-CP=lambda mb: pltpu.CompilerParams(vmem_limit_bytes=mb<<20)
-S=jax.ShapeDtypeStruct
-def normed(h):
-    wide=h.astype(f32)
-    return (wide*lax.rsqrt(jnp.mean(wide*wide,-1,keepdims=True)+1e-6)).astype(bf)
-def cost(n): return pl.CostEstimate(flops=2*M*D*F*n,bytes_accessed=1<<PAD,transcendentals=0)
-
-def norm_kernel(h_ref,a_ref,at_ref):
-    a=normed(h_ref[ALLOF])
-    a_ref[ALLOF]=a
-    at_ref[ALLOF]=a.T
-def norm(h):
-    return pl.pallas_call(norm_kernel,grid=(M//BM,),in_specs=[pl.BlockSpec((BM,D),lambda i:(i,0))],
-        out_specs=[pl.BlockSpec((BM,D),lambda i:(i,0)),pl.BlockSpec((D,BM),lambda i:(0,i))],
-        out_shape=[S((M,D),bf),S((D,M),bf)],compiler_params=CP(32),name="norm")(h)
-
-def gu_kernel(a_ref,wg_ref,wu_ref,g_ref,u_ref,pt_ref):
-    for r in range(0,M,SUB):
-        rows=pl.ds(r,SUB)
-        g=dot(a_ref[rows,:],wg_ref[0])
-        u=dot(a_ref[rows,:],wu_ref[0])
-        s=jax.nn.sigmoid(g)
-        b=g*s
-        g_ref[0,rows,:]=u*(s+b*(1-s)); u_ref[0,rows,:]=b
-        pt_ref[:,rows]=(b*u).astype(bf).T
-def gate_up(l,a,wg,wu):
-    return pl.pallas_call(gu_kernel,grid=(NG,),in_specs=[pl.BlockSpec((M,D),lambda j:(0,0)),pl.BlockSpec((1,D,COLS),lambda j:(l*NG+j,0,0)),pl.BlockSpec((1,D,COLS),lambda j:(l*NG+j,0,0))],
-        out_specs=[pl.BlockSpec((1,M,COLS),lambda j:(j,0,0))]*2+[pl.BlockSpec((COLS,M),lambda j:(j,0))],
-        out_shape=[S((NG,M,COLS),f32)]*2+[S((F,M),bf)],compiler_params=CP(60),cost_estimate=cost(2),name="gate_up")(a,wg,wu)
-
-def compact_kernel(w_ref,o_ref):
-    def group(k,c):
-        v=w_ref[0,pl.ds(k*8,8)].astype(f32)
-        o_ref[pl.ds(pl.multiple_of(k*GROUP,GROUP),GROUP),:]=jnp.concatenate([v[d,0:ROWS] for d in range(8)],0).astype(bf)
-        return c
-    lax.fori_loop(0,16,group,0)
-def compact(w):
-    n=w.shape[0]//2
-    return [pl.pallas_call(compact_kernel,grid=(n,),in_specs=[pl.BlockSpec((1,LANES,PAD,LANES),lambda k:(l*n+k,0,0,0))],
-        out_specs=pl.BlockSpec((F,LANES),lambda k:(0,k)),out_shape=S((F,D),bf),compiler_params=CP(32),name="compact")(w) for l in range(2)]
-
-def down_kernel(pt_ref,w_ref,h_ref,h1_ref,a_ref,at_ref):
-    y=dot(pt_ref[ALLOF],w_ref[ALLOF],0,0).astype(bf)
-    h=h_ref[ALLOF]+y
-    h1_ref[ALLOF]=h
-    a=normed(h)
-    a_ref[ALLOF]=a
-    at_ref[ALLOF]=a.T
-def down(pt,w,h):
-    return pl.pallas_call(down_kernel,grid=(M//BM,),in_specs=[pl.BlockSpec((F,BM),lambda i:(0,i)),pl.BlockSpec((F,D),lambda i:(0,0)),pl.BlockSpec((BM,D),lambda i:(i,0))],
-        out_specs=[pl.BlockSpec((BM,D),lambda i:(i,0))]*2+[pl.BlockSpec((D,BM),lambda i:(0,i))],
-        out_shape=[S((M,D),bf)]*2+[S((D,M),bf)],compiler_params=CP(60),cost_estimate=cost(1),name="down")(pt,w,h)
-
 def wd_kernel(pt_ref,dh_ref,t_ref,acc):
     acc[ALLOF]=dot(pt_ref[ALLOF],dh_ref[ALLOF])
     def group(k,c):
@@ -398,19 +457,14 @@
 
 def step(x,dy,wg,wu,wd):
     x,dy=x[0],dy[0]
-    gg,gu,gd=gather(wg,wu,wd)
-    gg,gu=(t.reshape(2*NG,D,COLS) for t in (gg,gu))
-    down_w=compact(gd.reshape(16,LANES,PAD,LANES))
-    a0,at0=norm(x)
-    g0,u0,pt0=gate_up(0,a0,gg,gu)
-    h1,a1,at1=down(pt0,down_w[0],x)
-    g1,u1,pt1=gate_up(1,a1,gg,gu)
+    gg,gu,_,ga,gb,pt,at_,h1,wc=forward(x,wg,wu,wd)
+    gg,gu=(t.reshape(2*NG,D,256) for t in (gg,gu))
     dh=dy
     terms=[None,None]
-    for l,(g,u,pt,at,h) in ((1,(g1,u1,pt1,at1,h1)),(0,(g0,u0,pt0,at0,x))):
-        td=grad_down(pt,dh)
-        dg,du,tg,tu=grad_gate_up(dh,down_w[l],g,u,at)
-        terms[l]=(tg.reshape(NG,RING,RING,RING,2,8,COLS),tu.reshape(NG,RING,RING,RING,2,8,COLS),td.reshape(8,RING,RING,RING,2,PAD,LANES))
+    for l,h in ((1,h1),(0,x)):
+        td=grad_down(pt[l],dh)
+        dg,du,tg,tu=grad_gate_up(dh,wc[l],ga[l],gb[l],at_[l])
+        terms[l]=(tg.reshape(NG,4,4,4,2,8,256),tu.reshape(NG,4,4,4,2,8,256),td.reshape(8,4,4,4,2,24,128))
         dh=grad_h(l,dg,du,gg,gu,h,dh)
     og,ou,od=reduce_scatter(*zip(*terms,strict=True),2,F,D)
     return dh[None],og,ou,od

time: 615 us -> 581 us (0.945)
  Pallas kernels: 592 us -> 483 us
  local copies, waits for them, and re-layouts: 21.9 us -> 97.3 us
    pallas_call x7 -> x1, Pallas kernels: 246 us -> 138 us  [forward(): pl.pallas_call(f_kernel, out_shape=[S((ITEMS, *TORUS, R8, COLS), bf)] * 2...]
    squeeze x0 -> x4, local copies, waits for them, and re-layouts: none -> 92.8 us  [the longest x3 76 us: step(): dg, du, tg, tu = grad_gate_up(dh, wc[l], ga[l], gb[l], at_[l])]
    unnamed x16 -> x8, local copies, waits for them, and re-layouts: 21.9 us -> 4.46 us
where the time goes in v2:
time: 581 us
  Pallas kernels  483 us (83%)
  local copies, waits for them, and re-layouts  97.3 us (17%)
    pallas_call x1, Pallas kernels, reduce_scatter(): return tuple(f(*tg, *tu, *td))  140 us
    pallas_call x1, Pallas kernels, forward(): pl.pallas_call(f_kernel, out_shape=[S((ITEMS, *TORUS, R8, COLS), bf)] * 2...  138 us
    pallas_call x2, Pallas kernels, grad_gate_up(): pl.pallas_call(b1_kernel, grid=(NG + 1,), in_specs=[pl.BlockSpec((M, D),...  98.1 us
    squeeze x3, local copies, waits for them, and re-layouts, step(): dg, du, tg, tu = grad_gate_up(dh, wc[l], ga[l], gb[l], at_[l])  76 us
    pallas_call x2, Pallas kernels, grad_h(): pl.pallas_call(b2_kernel, grid=(M // BM,), in_specs=[blk, blk, w, w, row,...  66.8 us
    pallas_call x2, Pallas kernels, grad_down(): pl.pallas_call(wd_kernel, grid=(D // COLS,), in_specs=[pl.BlockSpec((F, M...  40.4 us
    squeeze x1, local copies, waits for them, and re-layouts, step(): td = grad_down(pt[l], dh)  16.8 us

profile of v2, /device:TPU:0, one launch (start us, length us, event | category | flops | bytes accessed | tf_op | source)
XLA Modules:
  0.0 580.8 jit_solution(12728185744209221103)
XLA Ops:
  0.6 1.5 copy.9.wd
  2.2 137.6 %forward.1 = (bf16[22,4,4,4,2,8,256]{6,5,4,3,2,1,0:T(8,128)(2,1)}, bf16[22,4,4,4,2,8,256]{6,5,4,3,2,1,0:T(8,128)(2,1)}, bf16[16,4,4,4,2,24,128]{6,5,4,3,2,1,0:T(...) custom-call(bf16[2048,1024]{1,0:T(8,128)(2,1)} %bitcast.37, ...), custom_call_target="tpu_custom_call" | custom-call | tf_op jit(solution)/shard_map/forward/pallas_call | solution.py:239
  139.8 60.0 %slice_bitcast_fusion = (f32[11,2048,256]{2,1,0:T(8,128)}, f32[11,2048,256]{2,1,0:T(8,128)}, f32[11,2048,256]{2,1,0:T(8,128)}, f32[11,2048,256]{2,1,0:T(8,128)}) fusion(f32[2,11,2048,256]{3,2,1,0:T(8,128)} %get-tuple-element.25, f32[2,11,2048,256]{3,2,1,0:T(8,128)} %get-tuple-element.24), kind=kLoop, calls=%fused_computation | loop fusion | bytes 184549376 | tf_op jit(solution)/shard_map/squeeze | solution.py:466
  199.8 9.9 %slice_bitcast_fusion.6 = (bf16[2816,1024]{1,0:T(8,128)(2,1)}, bf16[2816,1024]{1,0:T(8,128)(2,1)}) fusion(bf16[2,2816,1024]{2,1,0:T(8,128)(2,1)} %get-tuple-element.23), kind=kLoop, calls=%fused_computation.6 | loop fusion | bytes 23068672 | tf_op jit(solution)/shard_map/squeeze | solution.py:466
  209.6 6.1 %slice_bitcast_fusion.8 = (bf16[1024,2048]{1,0:T(8,128)(2,1)}, bf16[1024,2048]{1,0:T(8,128)(2,1)}) fusion(bf16[2,1024,2048]{2,1,0:T(8,128)(2,1)} %get-tuple-element.26), kind=kLoop, calls=%fused_computation.8 | loop fusion | bytes 16777216 | tf_op jit(solution)/shard_map/squeeze | solution.py:466
  215.8 49.1 %grad_gate_up.2 = (bf16[11,2048,256]{2,1,0:T(8,128)(2,1)}, bf16[11,2048,256]{2,1,0:T(8,128)(2,1)}, f32[11,1024,256]{2,1,0:T(8,128)}, f32[11,1024,256]{2,1,0:T(8,128)}) custom-call(bf16[2048,1024]{1,0:T(8,128)(2,1)} %bitcast.43, bf16[2816,1024]{1,0:T(8,128)(2,1)} %get-tuple-element.53.wd_ref, f32[11,2048,256]{2,1,0:T(8,128)} %get-tuple-element.56.g_ref, ...), custom_call_target="tpu_custom_call" | custom-call | flops 35433480192 | bytes 16777216 | tf_op jit(solution)/shard_map/grad_gate_up/pallas_call | solution.py:435
  264.9 33.2 %grad_h.2.dh_ref = bf16[2048,1024]{1,0:T(8,128)(2,1)} custom-call(bf16[11,2048,256]{2,1,0:T(8,128)(2,1)} %get-tuple-element.27.dg_ref, bf16[11,2048,256]{2,1,0:T(8,128)(2,1)} %get-tuple-element.28.du_ref, bf16[22,1024,256]{2,1,0:T(8,128)(2,1)} %bitcast.39, bf16[22,1024,256]{2,1,0:T(8,128)(2,1)} %bitcast.41, bf16[2048,1024]{1,0:T(8,128)(2,1)} %get-tuple-element.31.h_ref, ...), custom_call_target="tpu_custom_call" | custom-call | flops 23622320128 | bytes 16777216 | tf_op jit(solution)/shard_map/grad_h/pallas_call | solution.py:454
  298.1 16.8 %slice_bitcast_fusion.4 = (bf16[2816,2048]{1,0:T(8,128)(2,1)}, bf16[2816,2048]{1,0:T(8,128)(2,1)}) fusion(bf16[2,2816,2048]{2,1,0:T(8,128)(2,1)} %get-tuple-element.38), kind=kLoop, calls=%fused_computation.4 | loop fusion | bytes 46137344 | tf_op jit(solution)/shard_map/squeeze | solution.py:465
  314.9 20.2 %grad_down.2 = f32[8,128,24,128]{3,2,1,0:T(8,128)} custom-call(bf16[2816,2048]{1,0:T(8,128)(2,1)} %get-tuple-element.51.pt_ref, bf16[2048,1024]{1,0:T(8,128)(2,1)} %grad_h.2.dh_ref), custom_call_target="tpu_custom_call" | custom-call | flops 11811160064 | bytes 16777216 | tf_op jit(solution)/shard_map/grad_down/pallas_call | solution.py:407
  335.1 49.0 %grad_gate_up.3 = (bf16[11,2048,256]{2,1,0:T(8,128)(2,1)}, bf16[11,2048,256]{2,1,0:T(8,128)(2,1)}, f32[11,1024,256]{2,1,0:T(8,128)}, f32[11,1024,256]{2,1,0:T(8,128)}) custom-call(bf16[2048,1024]{1,0:T(8,128)(2,1)} %grad_h.2.dh_ref, bf16[2816,1024]{1,0:T(8,128)(2,1)} %get-tuple-element.52.wd_ref, f32[11,2048,256]{2,1,0:T(8,128)} %get-tuple-element.57.g_ref, ...), custom_call_target="tpu_custom_call" | custom-call | flops 35433480192 | bytes 16777216 | tf_op jit(solution)/shard_map/grad_gate_up/pallas_call | solution.py:435
  384.2 20.2 %grad_down.3 = f32[8,128,24,128]{3,2,1,0:T(8,128)} custom-call(bf16[2816,2048]{1,0:T(8,128)(2,1)} %get-tuple-element.50.pt_ref, bf16[2048,1024]{1,0:T(8,128)(2,1)} %bitcast.45), custom_call_target="tpu_custom_call" | custom-call | flops 11811160064 | bytes 16777216 | tf_op jit(solution)/shard_map/grad_down/pallas_call | solution.py:407
  404.4 139.9 %scatter.1 = (bf16[2,8,2816]{2,1,0:T(8,128)(2,1)}, bf16[2,8,2816]{2,1,0:T(8,128)(2,1)}, bf16[2,22,1024]{2,1,0:T(8,128)(2,1)}) custom-call(f32[11,4,4,4,2,8,256]{6,5,4,3,2,1,0:T(8,128)} %bitcast.35, f32[11,4,4,4,2,8,256]{6,5,4,3,2,1,0:T(8,128)} %bitcast.33, f32[11,4,4,4,2,8,256]{6,5,4,3,2,1,0:T(8,128)} %bitcast.36, f32[11,4,4,4,2,8,256]{6,5,4,3,2,1,0:T(8,128)} %bitcast.34, ...), custom_call_target="tpu_custom_call" | custom-call | tf_op jit(solution)/shard_map/scatter/pallas_call | solution.py:395
  544.3 1.6 copy.10
  546.0 0.0 copy-start.1
  546.0 0.0 copy-start
  546.0 33.5 %grad_h.3 = bf16[2048,1024]{1,0:T(8,128)(2,1)} custom-call(bf16[11,2048,256]{2,1,0:T(8,128)(2,1)} %get-tuple-element.32.dg_ref, bf16[11,2048,256]{2,1,0:T(8,128)(2,1)} %get-tuple-element.33.du_ref, bf16[22,1024,256]{2,1,0:T(8,128)(2,1)} %bitcast.40, bf16[22,1024,256]{2,1,0:T(8,128)(2,1)} %bitcast.42, bf16[2048,1024]{1,0:T(8,128)(2,1)} %bitcast.38, ...), custom_call_target="tpu_custom_call" | custom-call | flops 23622320128 | bytes 16777216 | tf_op jit(solution)/shard_map/grad_h/pallas_call | solution.py:454
  579.5 0.0 copy-done.1
  579.5 0.6 copy.13
  580.1 0.0 copy-done
  580.1 0.6 copy.14
Async XLA Ops:
  546.0 33.5 %copy-start.1 = (bf16[2,8,2816]{2,1,0:T(8,128)(2,1)S(1)}, bf16[2,8,2816]{2,1,0:T(8,128)(2,1)}, u32[]{:S(2)}) copy-start(bf16[2,8,2816]{2,1,0:T(8,128)(2,1)} %get-tuple-element.63) | copy-start | bytes 270340
  546.0 34.2 %copy-start = (bf16[2,8,2816]{2,1,0:T(8,128)(2,1)S(1)}, bf16[2,8,2816]{2,1,0:T(8,128)(2,1)}, u32[]{:S(2)}) copy-start(bf16[2,8,2816]{2,1,0:T(8,128)(2,1)} %get-tuple-element.64) | copy-start | bytes 270340

commit v3 on v0

v3 whole, which is shorter than its diff:
```python
import functools

import jax
import jax.numpy as jnp
from jax import lax
from jax.experimental import pallas as pl
from jax.experimental.pallas import tpu as pltpu
from jax.sharding import PartitionSpec as P

MESH=pl.DeviceIdType.MESH
bf=jnp.bfloat16
f32=jnp.float32
S=jax.ShapeDtypeStruct
ALLOF=...
ALL=slice(None)
M,D,F,L=2048,1024,2816,2
RING,COLS,LANES=4,256,128
CHIPS=(RING,)*3
TORUS=(*CHIPS,2)
R8,ROWS,PAD,EIGHT=8,22,24,8
GROUP=EIGHT*ROWS
NG,ND=F//COLS,D//LANES
ITEMS=L*NG
BM=256
TILES=M//BM
ORDERS=((2,1,0),(0,2,1),(1,0,2))
HALF_COLS=((pl.ds(0,R8),pl.ds(0,LANES)),(pl.ds(0,R8),pl.ds(LANES,LANES)))
HALF_ROWS=((pl.ds(0,16),pl.ds(0,LANES)),(pl.ds(16,8),pl.ds(0,LANES)))
DMA=pltpu.SemaphoreType.DMA
ANY=pl.BlockSpec(memory_space=pl.ANY)
INVMEM=pl.BlockSpec(memory_space=pltpu.VMEM)
VMEM=pltpu.VMEM

def dot(a,b,ca=1,cb=0):
    return lax.dot_general(a,b,(((ca,),(cb,)),((),())),preferred_element_type=f32)

def rms(h):
    return lax.rsqrt(jnp.mean(h*h,-1,keepdims=True)+1e-6)

def normed(h):
    wide=h.astype(f32)
    return (wide*rms(wide)).astype(bf)

def aligned(i,n):
    return pl.ds(pl.multiple_of(i*n,n),n)

def params(n,mb):
    return pltpu.CompilerParams(collective_id=n,has_side_effects=True,vmem_limit_bytes=mb<<20)


class Torus:
    def __init__(self):
        me=lax.axis_index("dp")
        chip,self.c=lax.div(me,2),lax.rem(me,2)
        self.xyz=(lax.div(chip,RING*RING),lax.rem(lax.div(chip,RING),RING),lax.rem(chip,RING))
        self.partner=me+1-2*self.c
        weight=(2*RING*RING,2*RING,2)
        sigma=1-2*self.c
        self.ring,self.ringid,self.p,self.q,self.pid,self.qid=[],[],[],[],[],[]
        for v,w in zip(self.xyz,weight,strict=True):
            place=lambda d: lax.rem(v+d,RING)
            ident=lambda u: me+(u-v)*w
            ring=[place(d) for d in range(1,RING)]
            p,q=place(RING+sigma),place(RING-sigma)
            for to,value in ((self.ring,ring),(self.ringid,[ident(u) for u in ring]),(self.p,p),(self.q,q),(self.pid,ident(p)),(self.qid,ident(q))):
                to.append(value)

    def barrier(self):
        b=pltpu.get_barrier_semaphore()
        reach=[to for ids in self.ringid for to in ids]+[self.partner]
        for to in reach:
            pl.semaphore_signal(b,inc=1,device_id={"dp":to},device_id_type=MESH)
        pl.semaphore_wait(b,len(reach))

def at(axis,v,axes=(0,1,2)):
    return tuple(v if k==axis else ALL for k in axes)

def remote(src,dst,sems,slot,k,to):
    send,recv=sems
    return pltpu.make_async_remote_copy(src_ref=src,dst_ref=dst,send_sem=send.at[slot,k],recv_sem=recv.at[slot,k],
        device_id={"dp":to},device_id_type=MESH)


SLOTS=4
G_OFF=(0,2,4,6,8,10,11)
G_DEPTH=G_OFF[-1]
DOWN_STEPS=TILES
F_STEPS=ITEMS+DOWN_STEPS

class Gather:
    def __init__(self,torus,order,g,own,halves,sems,local):
        self.t,self.order,self.g,self.own,self.halves,self.sems,self.local=torus,order,g,own,halves,sems,local
    def region(self,i,full,axis=None,v=None,part=(ALL,ALL)):
        where=(ALL if k in full else v if k==axis else self.t.xyz[k] for k in range(3))
        return self.g.at[(i,*where,self.t.c,*part)]
    def copies(self,stage,i):
        t=self.t
        a,b,last=self.order
        copy=lambda k,src,dst,to: remote(src,dst,self.sems,lax.rem(i,SLOTS),k,to)
        if stage==0:
            mine=self.region(i,())
            return [copy(k,self.own(i),mine,to) for k,to in enumerate(t.ringid[a])]
        if stage==5:
            mine=self.region(i,(0,1,2))
            return [copy(11,mine,mine,t.partner)]
        axis,full,k=(b,(a,),3) if stage<3 else (last,(a,b),7)
        to=(t.pid[axis],t.qid[axis])
        if stage%2:
            mine=self.region(i,full)
            return [copy(k+d,mine,mine,to[d]) for d in range(2)]
        came=(t.q[axis],t.p[axis])
        parts=[self.region(i,full,axis,came[d],self.halves[d]) for d in range(2)]
        return [copy(k+2+d,parts[d],parts[d],to[d]) for d in range(2)]
    def own_copy(self,i):
        return pltpu.make_async_copy(self.own(i),self.region(i,()),self.local.at[lax.rem(i,SLOTS)])
    def run(self,stage,i):
        if stage>0:
            for cp in self.copies(stage-1,i): cp.wait()
            if stage==1: self.own_copy(i).wait()
        if stage<6:
            for cp in self.copies(stage,i): cp.start()
            if stage==0: self.own_copy(i).start()

def f_kernel(x,wg,wu,wd,gg,gu,gd,ga,gb,pt,at_,h1,wc,
        wdp,xv,av,ptv,wcv,wv,dv,abv,atv,hv,xsem,wsem,dsem,absem,ptsem,atsem,hsem,wcsem,*gsems):
    for l in range(L):
        wdp[l,0:ROWS,:]=wd[l]
        wdp[l,ROWS:PAD,:]=jnp.zeros((PAD-ROWS,D),bf)
    load_x=pltpu.make_async_copy(x,xv,xsem)
    load_x.start()
    torus=Torus()
    torus.barrier()
    own_g=lambda i: wg.at[lax.div(i,NG),:,aligned(lax.rem(i,NG),COLS)]
    own_u=lambda i: wu.at[lax.div(i,NG),:,aligned(lax.rem(i,NG),COLS)]
    own_d=lambda k: wdp.at[lax.div(k,ND),:,aligned(lax.rem(k,ND),LANES)]
    eg=Gather(torus,ORDERS[0],gg,own_g,HALF_COLS,gsems[0:2],gsems[2])
    eu=Gather(torus,ORDERS[1],gu,own_u,HALF_COLS,gsems[3:5],gsems[5])
    ed=Gather(torus,ORDERS[2],gd,own_d,HALF_ROWS,gsems[6:8],gsems[8])
    def load_d(k):
        return pltpu.make_async_copy(gd.at[k],dv.at[lax.rem(k,2)],dsem.at[lax.rem(k,2)])
    def store_wc(l):
        return pltpu.make_async_copy(wcv.at[l],wc.at[l],wcsem.at[l])
    def compact(k):
        load_d(k).wait()
        def group(j,carry):
            v=dv[lax.rem(k,2),lax.div(j,RING),lax.rem(j,RING)].reshape(EIGHT,PAD,LANES).astype(f32)
            wcv[lax.div(k,ND),aligned(j,GROUP),aligned(lax.rem(k,ND),LANES)]=jnp.concatenate([v[d,0:ROWS] for d in range(EIGHT)],0).astype(bf)
            return carry
        lax.fori_loop(0,16,group,0)
        @pl.when(lax.rem(k,ND)==ND-1)
        def _(): store_wc(lax.div(k,ND)).start()
    def tick(t):
        i=t-G_DEPTH-1
        @pl.when((i>=0)&(i<L*ND))
        def _(): compact(i)
        for stage in reversed(range(7)):
            i=t-G_OFF[stage]
            @pl.when((i>=0)&(i<ITEMS))
            def _():
                eg.run(stage,i); eu.run(stage,i)
                @pl.when(i<L*ND)
                def _():
                    ed.run(stage,i)
                    if stage==6: load_d(i).start()
    item_of=lambda k: jnp.where(k<NG,k,k-DOWN_STEPS)
    is_item=lambda k: ((k>=0)&(k<NG))|((k>=NG+DOWN_STEPS)&(k<F_STEPS))
    def load_w(i):
        return [pltpu.make_async_copy(g.at[i],wv.at[m,lax.rem(i,2)],wsem.at[m,lax.rem(i,2)]) for m,g in enumerate((gg,gu))]
    def store_ab(i):
        s=lax.rem(i,2)
        return [pltpu.make_async_copy(abv.at[m,s],o.at[lax.div(i,NG),lax.rem(i,NG)],absem.at[m,s]) for m,o in enumerate((ga,gb))]+[
            pltpu.make_async_copy(ptv.at[:,aligned(lax.rem(i,NG),COLS)],pt.at[lax.div(i,NG),:,aligned(lax.rem(i,NG),COLS)],ptsem.at[s])]
    def store_at(l,r):
        return pltpu.make_async_copy(atv.at[lax.rem(r,2)],at_.at[l,:,aligned(r,BM)],atsem.at[lax.rem(r,2)])
    def store_h(r):
        return pltpu.make_async_copy(hv.at[lax.rem(r,2)],h1.at[aligned(r,BM)],hsem.at[lax.rem(r,2)])
    def put_a(l,r,h):
        a=normed(h)
        av[aligned(r,BM),:]=a
        @pl.when(r>=2)
        def _(): store_at(l,r-2).wait()
        atv[lax.rem(r,2)]=a.T
        store_at(l,r).start()
    def gate_up(i):
        for cp in load_w(i): cp.wait()
        @pl.when(i>=2)
        def _():
            for cp in store_ab(i-2): cp.wait()
        s=lax.rem(i,2)
        w_gate,w_up=(wv[m,s].reshape(D,COLS) for m in range(2))
        for r in range(TILES):
            rows=pl.ds(r*BM,BM)
            g=dot(av[rows,:],w_gate)
            u=dot(av[rows,:],w_up)
            sg=jax.nn.sigmoid(g)
            b=g*sg
            abv[0,s,rows,:]=u*(sg+b*(1-sg))
            abv[1,s,rows,:]=b
            ptv[r,aligned(lax.rem(i,NG),COLS),:]=(b*u).astype(bf).T
        for cp in store_ab(i): cp.start()
    def down(r):
        y=dot(ptv[r],wcv[0],0,0).astype(bf)
        h=xv[aligned(r,BM),:]+y
        @pl.when(r>=2)
        def _(): store_h(r-2).wait()
        hv[lax.rem(r,2)]=h
        store_h(r).start()
        put_a(1,r,h)
    tick(0)
    load_x.wait()
    def norm(r,carry):
        put_a(0,r,xv[aligned(r,BM),:])
        return carry
    lax.fori_loop(0,TILES,norm,0)
    for r in (TILES-2,TILES-1): store_at(0,r).wait()
    def step(t,carry):
        k=t-G_DEPTH-1
        tick(t)
        @pl.when(is_item(k+1))
        def _():
            for cp in load_w(item_of(k+1)): cp.start()
        @pl.when(is_item(k))
        def _(): gate_up(item_of(k))
        @pl.when((k>=NG)&(k<NG+DOWN_STEPS))
        def _(): down(k-NG)
        return carry
    lax.fori_loop(1,F_STEPS+G_DEPTH+1,step,0)
    for r in (TILES-2,TILES-1):
        store_at(1,r).wait()
        store_h(r).wait()
    for i in (ITEMS-2,ITEMS-1):
        for cp in store_ab(i): cp.wait()
    for l in range(L): store_wc(l).wait()

def forward(x,wg,wu,wd):
    return pl.pallas_call(f_kernel,
        out_shape=[S((ITEMS,*TORUS,R8,COLS),bf)]*2+[S((L*ND,*TORUS,PAD,LANES),bf)]+[S((L,NG,M,COLS),f32)]*2+[
            S((L,TILES,F,BM),bf),S((L,D,M),bf),S((M,D),bf),S((L,F,D),bf)],
        in_specs=[ANY]+[INVMEM]*3,out_specs=[ANY]*9,
        scratch_shapes=[VMEM((L,PAD,D),bf),VMEM((M,D),bf),VMEM((M,D),bf),VMEM((TILES,F,BM),bf),VMEM((L,F,D),bf),VMEM((2,2,*TORUS,R8,COLS),bf),
            VMEM((2,*TORUS,PAD,LANES),bf),VMEM((2,2,M,COLS),f32),VMEM((2,D,BM),bf),VMEM((2,BM,D),bf),
            DMA,DMA((2,2)),DMA((2,)),DMA((2,2)),DMA((2,)),DMA((2,)),DMA((2,)),DMA((L,))]+[DMA((SLOTS,12)),DMA((SLOTS,12)),DMA((SLOTS,))]*3,
        compiler_params=params(0,62),name="forward")(x,wg,wu,wd)


B_TAIL=NG+1
B_STEPS=B_TAIL+TILES
SEND,DOWN=2,2
S_STAGES=7

class Scatter:
    @staticmethod
    def scratch(rows,n,halves,own=4,ds=2):
        V=lambda *s: VMEM((2,*s),bf)
        A,B=((r.size,c.size) for r,c in halves)
        plane,line=(RING,RING),(RING,)
        return [VMEM((own,*CHIPS,rows,n),f32),VMEM((ds,*CHIPS,rows,n),bf),V(*CHIPS,rows,n),
            V(*plane,rows,n),V(*plane,*A),V(*plane,*B),V(2,*plane,rows,n),V(2,*plane,rows,n),VMEM((2,*plane,rows,n),f32),
            V(*line,rows,n),V(*line,*A),V(*line,*B),V(2,*line,rows,n),V(2,*line,rows,n),VMEM((2,*line,rows,n),f32),
            V(3,rows,n),V(3,rows,n),DMA((2,12)),DMA((2,12))]
    COUNT=19
    def __init__(self,torus,order,out,halves,refs):
        self.t,self.order,self.out,self.halves=torus,order,out,halves
        (self.own,self.ds,self.dr,self.a1s,self.a1A,self.a1B,self.a2s,self.a2r,self.t1,
            self.b1s,self.b1A,self.b1B,self.b2s,self.b2r,self.t2,self.cs,self.cr,*self.sems)=refs
    @staticmethod
    def slot(ref,i):
        return lax.rem(i,ref.shape[0])
    def copies(self,stage,i):
        t=self.t
        first,b,a=self.order
        s=lax.rem(i,2)
        copy=lambda k,src,dst,to: remote(src,dst,self.sems,s,k,to)
        if stage==0: return [copy(0,self.ds.at[self.slot(self.ds,i)],self.dr.at[s],t.partner)]
        if stage==5: return [copy(9+d,self.cs.at[s,d],self.cr.at[s,d],to) for d,to in enumerate(t.ringid[first])]
        axis,k=(a,1) if stage<3 else (b,5)
        if stage%2:
            src,A,B=(self.a1s,self.a1A,self.a1B) if stage<3 else (self.b1s,self.b1A,self.b1B)
            lead=(ALL,)*(len(A.shape)-3)
            pieces=[(src.at[(s,*lead,*h)],dst.at[s]) for h,dst in zip(self.halves,(A,B),strict=True)]
        else:
            src,dst=(self.a2s,self.a2r) if stage<3 else (self.b2s,self.b2r)
            pieces=[(src.at[s,d],dst.at[s,d]) for d in range(2)]
            k+=2
        return [copy(k+d,*piece,to) for d,(piece,to) in enumerate(zip(pieces,(t.pid[axis],t.qid[axis]),strict=True))]
    def run(self,stage,i,column):
        t=self.t
        first,b,a=self.order
        s,o=lax.rem(i,2),self.slot(self.own,i)
        if stage>0:
            for cp in self.copies(stage-1,i): cp.wait()
        rem=[k for k in range(3) if k!=a]
        plane=lambda v: self.own[(o,*at(a,v))]
        line=lambda v: self.t1[(s,*at(b,v,rem))]
        axis,get=(a,plane) if stage<3 else (b,line)
        if stage==1:
            self.own[o]+=self.dr[s].astype(f32)
            self.a1s[s]=plane(t.ring[a][1]).astype(bf)
        elif stage==3:
            self.t1[s]=plane(t.xyz[a])+self.a2r[s,0].astype(f32)+self.a2r[s,1].astype(f32)
            self.b1s[s]=line(t.ring[b][1]).astype(bf)
        elif stage in (2,4):
            dst,came=(self.a2s,(self.a1A,self.a1B)) if stage==2 else (self.b2s,(self.b1A,self.b1B))
            for d,to in enumerate((t.p[axis],t.q[axis])):
                v=get(to)
                lead=(ALL,)*(v.ndim-2)
                for e,(r,c) in enumerate(self.halves):
                    part=v[(*lead,slice(r.start,r.start+r.size),slice(c.start,c.start+c.size))]
                    if d==e: part=part+came[e][s].astype(f32)
                    dst[(s,d,*lead,r,c)]=part.astype(bf)
        elif stage==5:
            self.t2[s]=line(t.xyz[b])+self.b2r[s,0].astype(f32)+self.b2r[s,1].astype(f32)
            for d,to in enumerate(t.ring[first]):
                self.cs[s,d]=self.t2[s,to].astype(bf)
        elif stage==6:
            v=self.t2[s,t.xyz[first]]
            for d in range(3): v=v+self.cr[s,d].astype(f32)
            self.out(column,v.astype(bf))
        if stage<6:
            for cp in self.copies(stage,i): cp.start()

def split(core,v0,v1):
    return jnp.where(core==0,v0,v1),jnp.where(core==0,v1,v0)

def b_kernel(x,dy,h1,ga,gb,pt,at_,wc,gg,gu,dx,og,ou,od,dgo,duo,
        odp,dhv,atv,both,abv,gsv,wdv,tiles,hv,dhsem,atsem,bothsem,absem,gssem,wdsem,tilesem,hsem,dxsem,*scr):
    torus=Torus()
    layer_of=lambda half: L-1-half
    def prefetch(half,j):
        l,s=layer_of(half),lax.rem(j,2)
        return [pltpu.make_async_copy(o.at[l,j],abv.at[m,s],absem.at[m,s]) for m,o in enumerate((ga,gb))]+[
            pltpu.make_async_copy(wc.at[l,aligned(j,COLS)],wdv.at[s],wdsem.at[s])]
    def load_at(half):
        return pltpu.make_async_copy(at_.at[layer_of(half)],atv,atsem)
    def load_pt(half):
        return [pltpu.make_async_copy(pt.at[aligned(layer_of(half),TILES*F)],both,bothsem.at[0])]
    def load_w(half):
        return [pltpu.make_async_copy(g.at[aligned(layer_of(half),NG*D)],both.at[pl.ds(m*NG*D,NG*D)],bothsem.at[m]) for m,g in enumerate((gg,gu))]
    def store_gs(j):
        s=lax.rem(j,2)
        return [pltpu.make_async_copy(gsv.at[m,s],o.at[j],gssem.at[m,s]) for m,o in enumerate((dgo,duo))]
    def load_tile(r):
        s=lax.rem(r,2)
        return [pltpu.make_async_copy(o.at[:,aligned(r,BM)],tiles.at[m,s],tilesem.at[m,s]) for m,o in enumerate((dgo,duo))]
    def load_h(half,r,go):
        s=lax.rem(r,2)
        for k,h in enumerate((h1,x)):
            @pl.when(half==k)
            def _():
                cp=pltpu.make_async_copy(h.at[aligned(r,BM)],hv.at[s],hsem.at[s])
                cp.start() if go else cp.wait()
    def store_dx(r):
        return pltpu.make_async_copy(dhv.at[aligned(r,BM)],dx.at[aligned(r,BM)],dxsem.at[r])
    def each(copies,go):
        for cp in copies: cp.start() if go else cp.wait()

    load_dh=pltpu.make_async_copy(dy,dhv,dhsem)
    load_dh.start()
    each(prefetch(0,0),True)
    load_at(0).start()
    torus.barrier()
    n=Scatter.COUNT
    def outs(half):
        l=layer_of(half)
        def gate(j,v): og[l,:,aligned(j,COLS)]=v
        def up(j,v): ou[l,:,aligned(j,COLS)]=v
        def down(k,v): odp[l,:,aligned(k,LANES)]=v
        return gate,up,down
    def scatters(half):
        return [Scatter(torus,order,out,h,scr[m*n:(m+1)*n]) for m,(order,out,h) in
            enumerate(zip(ORDERS,outs(half),(HALF_COLS,HALF_COLS,HALF_ROWS),strict=True))]
    eg,eu,ed=scatters(0)

    def tick(half,s):
        eg,eu,ed=scatters(half)
        for stage in reversed(range(S_STAGES)):
            j=s-SEND-stage
            @pl.when((j>=0)&(j<NG))
            def _():
                for e in (eg,eu): e.run(stage,half*NG+j,j)
                @pl.when((j>=DOWN)&(j<DOWN+ND))
                def _(): ed.run(stage,half*ND+j-DOWN,j-DOWN)

    def front(j):
        s=lax.rem(j,2)
        for r in range(TILES):
            rows=pl.ds(r*BM,BM)
            dp=dot(dhv[rows,:],wdv[s],1,1).astype(bf).astype(f32)
            for m in range(2):
                gsv[m,s,rows,:]=(dp*abv[m,s,rows,:]).astype(bf)
    def back(half,j):
        s,i=lax.rem(j,2),half*NG+j
        o,to=Scatter.slot(eg.own,i),Scatter.slot(eg.ds,i)
        for m,e in enumerate((eg,eu)):
            grad=gsv[m,s]
            for k in range(RING):
                v=dot(atv[pl.ds(k*BM,BM),:],grad).reshape(RING*RING,2,R8,COLS)
                own,other=split(torus.c,v[:,0],v[:,1])
                e.own[o,k]=own.reshape(RING,RING,R8,COLS)
                e.ds[to,k]=other.astype(bf).reshape(RING,RING,R8,COLS)
    def grad_down(half,k):
        dh=dhv[:,aligned(lax.div(k,2),COLS)]
        first=half*ND+k
        for g in range(RING*RING):
            rows=jnp.concatenate([both[pl.ds(r*F+g*GROUP,GROUP),:] for r in range(TILES)],1)
            v=dot(rows,dh)
            for z in range(RING):
                pair=[v[ROWS*d:ROWS*d+ROWS] for d in (2*z,2*z+1)]
                own,other=split(torus.c,*pair)
                other=other.astype(bf)
                for e in range(2):
                    cols=slice(e*LANES,e*LANES+LANES)
                    ed.own[Scatter.slot(ed.own,first+e),g//RING,g%RING,z,0:ROWS,:]=own[:,cols]
                    ed.ds[Scatter.slot(ed.ds,first+e),g//RING,g%RING,z,0:ROWS,:]=other[:,cols]
    def grad_h(half,r):
        s=lax.rem(r,2)
        acc=None
        for j in range(NG):
            for m in range(2):
                v=dot(tiles[m,s,j],both[pl.ds((m*NG+j)*D,D),:],1,1)
                acc=v if acc is None else acc+v
        d=acc.astype(bf).astype(f32)
        h=hv[s].astype(f32)
        scale=rms(h)
        through=jnp.sum(d*h,-1,keepdims=True)*(scale*scale*scale)*(1/D)
        rows=aligned(r,BM)
        dhv[rows,:]=dhv[rows,:]+(d*scale-h*through).astype(bf)
        @pl.when(half==L-1)
        def _(): store_dx(r).start()

    load_dh.wait()
    def step(now,carry):
        half,s=lax.div(now,B_STEPS),lax.rem(now,B_STEPS)
        r=s-B_TAIL
        tick(half,s)
        @pl.when(s==0)
        def _(): each(load_pt(half),True)
        @pl.when(s<NG-1)
        def _(): each(prefetch(half,s+1),True)
        @pl.when(s==DOWN+ND)
        def _(): each(load_w(half),True)
        @pl.when(s==B_TAIL-1)
        def _():
            each(store_gs(NG-1),False)
            each(store_gs(NG-2),False)
            each(load_tile(0),True)
            load_h(half,0,True)
        @pl.when(s==B_TAIL)
        def _(): each(load_w(half),False)
        @pl.when((s==B_TAIL)&(half<L-1))
        def _(): load_at(half+1).start()
        @pl.when((s>=B_TAIL)&(s<B_STEPS-1))
        def _():
            each(load_tile(r+1),True)
            load_h(half,r+1,True)
        @pl.when((s==B_STEPS-1)&(half<L-1))
        def _(): each(prefetch(half+1,0),True)
        @pl.when(s<NG)
        def _():
            each(prefetch(half,s),False)
            @pl.when(s>=2)
            def _(): each(store_gs(s-2),False)
        @pl.when(s==1)
        def _(): load_at(half).wait()
        @pl.when(s==DOWN)
        def _(): each(load_pt(half),False)
        @pl.when(s>=B_TAIL)
        def _():
            each(load_tile(r),False)
            load_h(half,r,False)
        @pl.when((s>=DOWN)&(s<DOWN+ND)&(lax.rem(s,2)==0))
        def _(): grad_down(half,s-DOWN)
        @pl.when(s==0)
        def _(): front(s)
        @pl.when((s>0)&(s<NG))
        def _():
            front(s); back(half,s-1)
        @pl.when(s==NG)
        def _(): back(half,s-1)
        @pl.when(s<NG)
        def _(): each(store_gs(s),True)
        @pl.when(s>=B_TAIL)
        def _(): grad_h(half,r)
        return carry
    lax.fori_loop(0,L*B_STEPS,step,0)
    for r in range(TILES): store_dx(r).wait()
    od[...]=odp[:,0:ROWS,:]

def backward(x,dy,h1,ga,gb,pt,at_,wc,gg,gu):
    return pl.pallas_call(b_kernel,
        out_shape=[S((M,D),bf),S((L,R8,F),bf),S((L,R8,F),bf),S((L,ROWS,D),bf)]+[S((NG,M,COLS),bf)]*2,
        in_specs=[ANY]*10,out_specs=[ANY]+[INVMEM]*3+[ANY]*2,
        scratch_shapes=[VMEM((L,PAD,D),bf),VMEM((M,D),bf),VMEM((D,M),bf),VMEM((TILES*F,COLS),bf),VMEM((2,2,M,COLS),f32),VMEM((2,2,M,COLS),bf),
            VMEM((2,COLS,D),bf),VMEM((2,2,NG,BM,COLS),bf),VMEM((2,BM,D),bf),
            DMA,DMA,DMA((2,)),DMA((2,2)),DMA((2,2)),DMA((2,)),DMA((2,2)),DMA((2,)),DMA((TILES,))]
            +Scatter.scratch(R8,COLS,HALF_COLS)*2+Scatter.scratch(PAD,LANES,HALF_ROWS,6,4),
        compiler_params=params(1,63),name="backward")(x,dy,h1,ga,gb,pt,at_,wc,gg,gu)

def step(x,dy,wg,wu,wd):
    x,dy=x[0],dy[0]
    gg,gu,_,ga,gb,pt,at_,h1,wc=forward(x,wg,wu,wd)
    gg,gu=(t.reshape(ITEMS*D,COLS) for t in (gg,gu))
    dx,og,ou,od,_,_=backward(x,dy,h1,ga,gb,pt.reshape(L*TILES*F,COLS),at_,wc,gg,gu)
    return dx[None],og,ou,od

def solution(mesh):
    tok=P(("rep","dp"),None,None)
    w=P(None,"dp",None)
    o=P("rep","dp",None)
    return jax.shard_map(step,mesh=mesh,in_specs=(tok,tok,w,w,w),out_specs=(tok,o,o,o),check_vma=False)
```

time: 3090 us -> 360 us (0.12)
  waiting for transfers between devices: 2170 us -> 0 us
  blocking collectives: 368 us -> 0 us
  Pallas kernels: 0 us -> 348 us
  matrix products: 344 us -> 0 us
  other arithmetic: 80.2 us -> 0 us
  starting transfers between devices: 69.3 us -> 0 us
    unnamed x36 -> x0, waiting for transfers between devices: 1910 us -> none
    unnamed x1 -> x0, blocking collectives: 368 us -> none
    pallas_call x0 -> x2, Pallas kernels: none -> 348 us  [the longest x1 212 us: backward(): pl.pallas_call(b_kernel, out_shape=[S((M, D), bf), S((L, R8, F), bf), S((...]
    dot_general x17 -> x0, matrix products: 344 us -> none  [the longest x6 126 us: layer(): up = jnp.dot(a, w['w_up'], preferred_element_type=jnp.float32)]
    squeeze x6 -> x0, waiting for transfers between devices: 259 us -> none  [stack(): h = layer(h, {name: w[number] for name, w in weights.items()})]
    unnamed x26 -> x0, starting transfers between devices: 69 us -> none
    unnamed x5 -> x0, other arithmetic: 62.9 us -> none
  transfers between devices with their start and end apart: 32 -> 0, of which waited for: 9 -> 0; matrix products, arithmetic and copies ran while one was open for 27% -> 0% of each run, Pallas kernels for 0% -> 0%
where the time goes in v3:
time: 360 us
  Pallas kernels  348 us (97%)
  local copies, waits for them, and re-layouts  10.9 us (3%)
    pallas_call x1, Pallas kernels, backward(): pl.pallas_call(b_kernel, out_shape=[S((M, D), bf), S((L, R8, F), bf), S((...  212 us
    pallas_call x1, Pallas kernels, forward(): pl.pallas_call(f_kernel, out_shape=[S((ITEMS, *TORUS, R8, COLS), bf)] * 2...  136 us
    unnamed x5, local copies, waits for them, and re-layouts  10.9 us

profile of v3, /device:TPU:0, one launch (start us, length us, event | category | flops | bytes accessed | tf_op | source)
XLA Modules:
  0.0 359.7 jit_solution(17151018304849755480)
XLA Ops:
  0.6 1.5 copy.9.wd
  2.2 136.2 %forward.1 = (bf16[22,4,4,4,2,8,256]{6,5,4,3,2,1,0:T(8,128)(2,1)}, bf16[22,4,4,4,2,8,256]{6,5,4,3,2,1,0:T(8,128)(2,1)}, bf16[16,4,4,4,2,24,128]{6,5,4,3,2,1,0:T(...) custom-call(bf16[2048,1024]{1,0:T(8,128)(2,1)} %bitcast.7, ...), custom_call_target="tpu_custom_call" | custom-call | tf_op jit(solution)/shard_map/forward/pallas_call | solution.py:236
  138.4 212.0 %backward.1 = (bf16[2048,1024]{1,0:T(8,128)(2,1)}, bf16[2,8,2816]{2,1,0:T(8,128)(2,1)}, bf16[2,8,2816]{2,1,0:T(8,128)(2,1)}, bf16[2,22,1024]{2,1,0:T(8,128)(2,1)...) custom-call(bf16[2048,1024]{1,0:T(8,128)(2,1)} %bitcast.8, bf16[2048,1024]{1,0:T(8,128)(2,1)} %bitcast.12, ...), custom_call_target="tpu_custom_call" | custom-call | tf_op jit(solution)/shard_map/backward/pallas_call | solution.py:490
  350.4 1.6 copy.10
  352.0 4.6 %copy.14 = bf16[1,2048,1024]{2,1,0:T(8,128)(2,1)} copy(bf16[1,2048,1024]{2,1,0:T(8,128)(2,1)} %bitcast.11) | data formatting | bytes 8388608
  356.6 1.5 copy.15
  358.2 1.5 copy.16

commit v4 on v3

--- a/solution.py
+++ b/solution.py
@@ -82,49 +82,63 @@
 
 
 SLOTS=4
-G_OFF=(0,2,4,6,8,10,11)
+G_OFF=(0,2,4,6,8,9)
+G_LAST=len(G_OFF)-1
 G_DEPTH=G_OFF[-1]
-DOWN_STEPS=TILES
+DM=TILES//2*BM
+DOWN_STEPS=M//DM
 F_STEPS=ITEMS+DOWN_STEPS
 
 class Gather:
-    def __init__(self,torus,order,g,own,halves,sems,local):
-        self.t,self.order,self.g,self.own,self.halves,self.sems,self.local=torus,order,g,own,halves,sems,local
+    COPIES=11
+    def __init__(self,torus,order,g,own,shards,halves,sems,local):
+        self.t,self.order,self.g,self.own,self.shards,self.halves,self.sems,self.local=torus,order,g,own,shards,halves,sems,local
     def region(self,i,full,axis=None,v=None,part=(ALL,ALL)):
         where=(ALL if k in full else v if k==axis else self.t.xyz[k] for k in range(3))
         return self.g.at[(i,*where,self.t.c,*part)]
-    def copies(self,stage,i):
+    def pieces(self,stage,i):
         t=self.t
         a,b,last=self.order
-        copy=lambda k,src,dst,to: remote(src,dst,self.sems,lax.rem(i,SLOTS),k,to)
         if stage==0:
             mine=self.region(i,())
-            return [copy(k,self.own(i),mine,to) for k,to in enumerate(t.ringid[a])]
-        if stage==5:
+            return [(self.own(i),mine,to) for to in t.ringid[a]]
+        if stage==1:
+            mine=self.region(i,(a,))
+            return [(mine,mine,to) for to in t.ringid[b]]
+        if stage==4:
             mine=self.region(i,(0,1,2))
-            return [copy(11,mine,mine,t.partner)]
-        axis,full,k=(b,(a,),3) if stage<3 else (last,(a,b),7)
-        to=(t.pid[axis],t.qid[axis])
-        if stage%2:
-            mine=self.region(i,full)
-            return [copy(k+d,mine,mine,to[d]) for d in range(2)]
-        came=(t.q[axis],t.p[axis])
-        parts=[self.region(i,full,axis,came[d],self.halves[d]) for d in range(2)]
-        return [copy(k+2+d,parts[d],parts[d],to[d]) for d in range(2)]
-    def own_copy(self,i):
-        return pltpu.make_async_copy(self.own(i),self.region(i,()),self.local.at[lax.rem(i,SLOTS)])
+            return [(mine,mine,t.partner)]
+        to=(t.pid[last],t.qid[last])
+        if stage==2:
+            mine=self.region(i,(a,b))
+            return [(mine,mine,to[d]) for d in range(2)]
+        came=(t.q[last],t.p[last])
+        parts=[self.region(i,(a,b),last,came[d],self.halves[d]) for d in range(2)]
+        return [(parts[d],parts[d],to[d]) for d in range(2)]
+    def copies(self,stage,i,slot):
+        first=(0,3,6,8,10)[stage]
+        send,recv=self.sems
+        return [pltpu.make_async_remote_copy(src_ref=src,dst_ref=dst,send_sem=send.at[first+k],recv_sem=recv.at[slot,first+k],
+            device_id={"dp":to},device_id_type=MESH) for k,(src,dst,to) in enumerate(self.pieces(stage,i))]
+    def own_copy(self,i,slot):
+        return pltpu.make_async_copy(self.own(i),self.region(i,()),self.local.at[slot])
     def run(self,stage,i):
+        slot=lax.rem(i,SLOTS)
         if stage>0:
-            for cp in self.copies(stage-1,i): cp.wait()
-            if stage==1: self.own_copy(i).wait()
-        if stage<6:
-            for cp in self.copies(stage,i): cp.start()
-            if stage==0: self.own_copy(i).start()
+            for cp in self.copies(stage-1,i,slot): cp.wait_recv()
+            if stage==1: self.own_copy(i,slot).wait()
+        if stage<G_LAST:
+            for cp in self.copies(stage,i,slot): cp.start()
+            if stage==0: self.own_copy(i,slot).start()
+    def drain(self):
+        self.own=lambda i: self.shards
+        for stage in range(G_LAST):
+            for k,cp in enumerate(self.copies(stage,ALL,0)): cp.wait_send()
 
 def f_kernel(x,wg,wu,wd,gg,gu,gd,ga,gb,pt,at_,h1,wc,
         wdp,xv,av,ptv,wcv,wv,dv,abv,atv,hv,xsem,wsem,dsem,absem,ptsem,atsem,hsem,wcsem,*gsems):
     for l in range(L):
-        wdp[l,0:ROWS,:]=wd[l]
+        wdp[l,0:ROWS,:]=wd[:,l,:]
         wdp[l,ROWS:PAD,:]=jnp.zeros((PAD-ROWS,D),bf)
     load_x=pltpu.make_async_copy(x,xv,xsem)
     load_x.start()
@@ -133,27 +147,28 @@
     own_g=lambda i: wg.at[lax.div(i,NG),:,aligned(lax.rem(i,NG),COLS)]
     own_u=lambda i: wu.at[lax.div(i,NG),:,aligned(lax.rem(i,NG),COLS)]
     own_d=lambda k: wdp.at[lax.div(k,ND),:,aligned(lax.rem(k,ND),LANES)]
-    eg=Gather(torus,ORDERS[0],gg,own_g,HALF_COLS,gsems[0:2],gsems[2])
-    eu=Gather(torus,ORDERS[1],gu,own_u,HALF_COLS,gsems[3:5],gsems[5])
-    ed=Gather(torus,ORDERS[2],gd,own_d,HALF_ROWS,gsems[6:8],gsems[8])
+    eg=Gather(torus,ORDERS[0],gg,own_g,wg,HALF_COLS,gsems[0:2],gsems[2])
+    eu=Gather(torus,ORDERS[1],gu,own_u,wu,HALF_COLS,gsems[3:5],gsems[5])
+    ed=Gather(torus,ORDERS[2],gd,own_d,wdp,HALF_ROWS,gsems[6:8],gsems[8])
     def load_d(k):
         return pltpu.make_async_copy(gd.at[k],dv.at[lax.rem(k,2)],dsem.at[lax.rem(k,2)])
     def store_wc(l):
         return pltpu.make_async_copy(wcv.at[l],wc.at[l],wcsem.at[l])
     def compact(k):
         load_d(k).wait()
-        def group(j,carry):
-            v=dv[lax.rem(k,2),lax.div(j,RING),lax.rem(j,RING)].reshape(EIGHT,PAD,LANES).astype(f32)
-            wcv[lax.div(k,ND),aligned(j,GROUP),aligned(lax.rem(k,ND),LANES)]=jnp.concatenate([v[d,0:ROWS] for d in range(EIGHT)],0).astype(bf)
+        def plane(x,carry):
+            for y in range(RING):
+                v=dv[lax.rem(k,2),x,y].reshape(EIGHT,PAD,LANES).astype(f32)
+                wcv[lax.div(k,ND),aligned(x*RING+y,GROUP),aligned(lax.rem(k,ND),LANES)]=jnp.concatenate([v[d,0:ROWS] for d in range(EIGHT)],0).astype(bf)
             return carry
-        lax.fori_loop(0,16,group,0)
+        lax.fori_loop(0,RING,plane,0)
         @pl.when(lax.rem(k,ND)==ND-1)
         def _(): store_wc(lax.div(k,ND)).start()
     def tick(t):
         i=t-G_DEPTH-1
         @pl.when((i>=0)&(i<L*ND))
         def _(): compact(i)
-        for stage in reversed(range(7)):
+        for stage in reversed(range(G_LAST+1)):
             i=t-G_OFF[stage]
             @pl.when((i>=0)&(i<ITEMS))
             def _():
@@ -161,7 +176,7 @@
                 @pl.when(i<L*ND)
                 def _():
                     ed.run(stage,i)
-                    if stage==6: load_d(i).start()
+                    if stage==G_LAST: load_d(i).start()
     item_of=lambda k: jnp.where(k<NG,k,k-DOWN_STEPS)
     is_item=lambda k: ((k>=0)&(k<NG))|((k>=NG+DOWN_STEPS)&(k<F_STEPS))
     def load_w(i):
@@ -171,16 +186,13 @@
         return [pltpu.make_async_copy(abv.at[m,s],o.at[lax.div(i,NG),lax.rem(i,NG)],absem.at[m,s]) for m,o in enumerate((ga,gb))]+[
             pltpu.make_async_copy(ptv.at[:,aligned(lax.rem(i,NG),COLS)],pt.at[lax.div(i,NG),:,aligned(lax.rem(i,NG),COLS)],ptsem.at[s])]
     def store_at(l,r):
-        return pltpu.make_async_copy(atv.at[lax.rem(r,2)],at_.at[l,:,aligned(r,BM)],atsem.at[lax.rem(r,2)])
+        return pltpu.make_async_copy(atv.at[r],at_.at[l,:,aligned(r,DM)],atsem.at[r])
     def store_h(r):
-        return pltpu.make_async_copy(hv.at[lax.rem(r,2)],h1.at[aligned(r,BM)],hsem.at[lax.rem(r,2)])
-    def put_a(l,r,h):
+        return pltpu.make_async_copy(hv.at[r],h1.at[aligned(r,DM)],hsem.at[r])
+    def put_a(slot,tile,first,h):
         a=normed(h)
-        av[aligned(r,BM),:]=a
-        @pl.when(r>=2)
-        def _(): store_at(l,r-2).wait()
-        atv[lax.rem(r,2)]=a.T
-        store_at(l,r).start()
+        av[pl.ds(first,BM),:]=a
+        atv[slot,:,pl.ds(tile*BM,BM)]=a.T
     def gate_up(i):
         for cp in load_w(i): cp.wait()
         @pl.when(i>=2)
@@ -199,20 +211,26 @@
             ptv[r,aligned(lax.rem(i,NG),COLS),:]=(b*u).astype(bf).T
         for cp in store_ab(i): cp.start()
     def down(r):
-        y=dot(ptv[r],wcv[0],0,0).astype(bf)
-        h=xv[aligned(r,BM),:]+y
-        @pl.when(r>=2)
-        def _(): store_h(r-2).wait()
-        hv[lax.rem(r,2)]=h
+        store_at(0,r).wait()
+        for tile in range(DM//BM):
+            first=pl.multiple_of(r*DM+tile*BM,BM)
+            y=dot(ptv[r*(DM//BM)+tile],wcv[0],0,0).astype(bf)
+            h=xv[pl.ds(first,BM),:]+y
+            hv[r,pl.ds(tile*BM,BM),:]=h
+            put_a(r,tile,first,h)
         store_h(r).start()
-        put_a(1,r,h)
+        store_at(1,r).start()
     tick(0)
     load_x.wait()
-    def norm(r,carry):
-        put_a(0,r,xv[aligned(r,BM),:])
-        return carry
-    lax.fori_loop(0,TILES,norm,0)
-    for r in (TILES-2,TILES-1): store_at(0,r).wait()
+    for r in range(DOWN_STEPS):
+        def norm(tile,carry):
+            first=pl.multiple_of(r*DM+tile*BM,BM)
+            a=normed(xv[pl.ds(first,BM),:])
+            av[pl.ds(first,BM),:]=a
+            atv[r,:,aligned(tile,BM)]=a.T
+            return carry
+        lax.fori_loop(0,DM//BM,norm,0)
+        store_at(0,r).start()
     def step(t,carry):
         k=t-G_DEPTH-1
         tick(t)
@@ -225,9 +243,10 @@
         def _(): down(k-NG)
         return carry
     lax.fori_loop(1,F_STEPS+G_DEPTH+1,step,0)
-    for r in (TILES-2,TILES-1):
+    for r in range(DOWN_STEPS):
         store_at(1,r).wait()
         store_h(r).wait()
+    for e in (eg,eu,ed): e.drain()
     for i in (ITEMS-2,ITEMS-1):
         for cp in store_ab(i): cp.wait()
     for l in range(L): store_wc(l).wait()
@@ -238,15 +257,15 @@
             S((L,TILES,F,BM),bf),S((L,D,M),bf),S((M,D),bf),S((L,F,D),bf)],
         in_specs=[ANY]+[INVMEM]*3,out_specs=[ANY]*9,
         scratch_shapes=[VMEM((L,PAD,D),bf),VMEM((M,D),bf),VMEM((M,D),bf),VMEM((TILES,F,BM),bf),VMEM((L,F,D),bf),VMEM((2,2,*TORUS,R8,COLS),bf),
-            VMEM((2,*TORUS,PAD,LANES),bf),VMEM((2,2,M,COLS),f32),VMEM((2,D,BM),bf),VMEM((2,BM,D),bf),
-            DMA,DMA((2,2)),DMA((2,)),DMA((2,2)),DMA((2,)),DMA((2,)),DMA((2,)),DMA((L,))]+[DMA((SLOTS,12)),DMA((SLOTS,12)),DMA((SLOTS,))]*3,
+            VMEM((2,*TORUS,PAD,LANES),bf),VMEM((2,2,M,COLS),f32),VMEM((DOWN_STEPS,D,DM),bf),VMEM((DOWN_STEPS,DM,D),bf),
+            DMA,DMA((2,2)),DMA((2,)),DMA((2,2)),DMA((2,)),DMA((DOWN_STEPS,)),DMA((DOWN_STEPS,)),DMA((L,))]+[DMA((Gather.COPIES,)),DMA((SLOTS,Gather.COPIES)),DMA((SLOTS,))]*3,
         compiler_params=params(0,62),name="forward")(x,wg,wu,wd)
 
 
 B_TAIL=NG+1
 B_STEPS=B_TAIL+TILES
 SEND,DOWN=2,2
-S_STAGES=7
+S_STAGES=6
 
 class Scatter:
     @staticmethod
@@ -254,15 +273,13 @@
         V=lambda *s: VMEM((2,*s),bf)
         A,B=((r.size,c.size) for r,c in halves)
         plane,line=(RING,RING),(RING,)
-        return [VMEM((own,*CHIPS,rows,n),f32),VMEM((ds,*CHIPS,rows,n),bf),V(*CHIPS,rows,n),
+        return [VMEM((own,*CHIPS,rows,n),f32),VMEM((ds,*CHIPS,rows,n),bf),VMEM((4,*CHIPS,rows,n),bf),
             V(*plane,rows,n),V(*plane,*A),V(*plane,*B),V(2,*plane,rows,n),V(2,*plane,rows,n),VMEM((2,*plane,rows,n),f32),
-            V(*line,rows,n),V(*line,*A),V(*line,*B),V(2,*line,rows,n),V(2,*line,rows,n),VMEM((2,*line,rows,n),f32),
-            V(3,rows,n),V(3,rows,n),DMA((2,12)),DMA((2,12))]
-    COUNT=19
+            V(3,*line,rows,n),V(3,*line,rows,n),VMEM((2,*line,rows,n),f32),V(3,rows,n),V(3,rows,n),DMA((2,Scatter.COPIES)),DMA((2,Scatter.COPIES))]
+    COUNT,COPIES=16,11
     def __init__(self,torus,order,out,halves,refs):
         self.t,self.order,self.out,self.halves=torus,order,out,halves
-        (self.own,self.ds,self.dr,self.a1s,self.a1A,self.a1B,self.a2s,self.a2r,self.t1,
-            self.b1s,self.b1A,self.b1B,self.b2s,self.b2r,self.t2,self.cs,self.cr,*self.sems)=refs
+        self.own,self.ds,self.dr,self.a1s,self.a1A,self.a1B,self.a2s,self.a2r,self.t1,self.bs,self.br,self.t2,self.cs,self.cr,*self.sems=refs
     @staticmethod
     def slot(ref,i):
         return lax.rem(i,ref.shape[0])
@@ -270,53 +287,43 @@
         t=self.t
         first,b,a=self.order
         s=lax.rem(i,2)
-        copy=lambda k,src,dst,to: remote(src,dst,self.sems,s,k,to)
-        if stage==0: return [copy(0,self.ds.at[self.slot(self.ds,i)],self.dr.at[s],t.partner)]
-        if stage==5: return [copy(9+d,self.cs.at[s,d],self.cr.at[s,d],to) for d,to in enumerate(t.ringid[first])]
-        axis,k=(a,1) if stage<3 else (b,5)
-        if stage%2:
-            src,A,B=(self.a1s,self.a1A,self.a1B) if stage<3 else (self.b1s,self.b1A,self.b1B)
-            lead=(ALL,)*(len(A.shape)-3)
-            pieces=[(src.at[(s,*lead,*h)],dst.at[s]) for h,dst in zip(self.halves,(A,B),strict=True)]
+        k=(0,1,3,5,8)[stage]
+        to=(t.pid[a],t.qid[a])
+        if stage==0: pieces=[(self.ds.at[self.slot(self.ds,i)],self.dr.at[self.slot(self.dr,i)],t.partner)]
+        elif stage==1: pieces=[(self.a1s.at[(s,ALL,ALL,*h)],dst.at[s],to[d]) for d,(h,dst) in enumerate(zip(self.halves,(self.a1A,self.a1B),strict=True))]
+        elif stage==2: pieces=[(self.a2s.at[s,d],self.a2r.at[s,d],to[d]) for d in range(2)]
         else:
-            src,dst=(self.a2s,self.a2r) if stage<3 else (self.b2s,self.b2r)
-            pieces=[(src.at[s,d],dst.at[s,d]) for d in range(2)]
-            k+=2
-        return [copy(k+d,*piece,to) for d,(piece,to) in enumerate(zip(pieces,(t.pid[axis],t.qid[axis]),strict=True))]
+            src,dst,ids=(self.bs,self.br,t.ringid[b]) if stage==3 else (self.cs,self.cr,t.ringid[first])
+            pieces=[(src.at[s,d],dst.at[s,d],ids[d]) for d in range(3)]
+        return [remote(src,dst,self.sems,s,k+d,dev) for d,(src,dst,dev) in enumerate(pieces)]
     def run(self,stage,i,column):
         t=self.t
         first,b,a=self.order
-        s,o=lax.rem(i,2),self.slot(self.own,i)
+        s,o,r=lax.rem(i,2),self.slot(self.own,i),self.slot(self.dr,i)
         if stage>0:
             for cp in self.copies(stage-1,i): cp.wait()
         rem=[k for k in range(3) if k!=a]
-        plane=lambda v: self.own[(o,*at(a,v))]
+        plane=lambda v: self.own[(o,*at(a,v))]+self.dr[(r,*at(a,v))].astype(f32)
         line=lambda v: self.t1[(s,*at(b,v,rem))]
-        axis,get=(a,plane) if stage<3 else (b,line)
+        came=lambda ref: (ref[s,d].astype(f32) for d in range(ref.shape[1]))
         if stage==1:
-            self.own[o]+=self.dr[s].astype(f32)
             self.a1s[s]=plane(t.ring[a][1]).astype(bf)
+        elif stage==2:
+            for d,to in enumerate((t.p[a],t.q[a])):
+                v=plane(to)
+                for e,(rows,cols) in enumerate(self.halves):
+                    part=v[:,:,rows.start:rows.start+rows.size,cols.start:cols.start+cols.size]
+                    if d==e: part=part+(self.a1A,self.a1B)[e][s].astype(f32)
+                    self.a2s[s,d,:,:,rows,cols]=part.astype(bf)
         elif stage==3:
-            self.t1[s]=plane(t.xyz[a])+self.a2r[s,0].astype(f32)+self.a2r[s,1].astype(f32)
-            self.b1s[s]=line(t.ring[b][1]).astype(bf)
-        elif stage in (2,4):
-            dst,came=(self.a2s,(self.a1A,self.a1B)) if stage==2 else (self.b2s,(self.b1A,self.b1B))
-            for d,to in enumerate((t.p[axis],t.q[axis])):
-                v=get(to)
-                lead=(ALL,)*(v.ndim-2)
-                for e,(r,c) in enumerate(self.halves):
-                    part=v[(*lead,slice(r.start,r.start+r.size),slice(c.start,c.start+c.size))]
-                    if d==e: part=part+came[e][s].astype(f32)
-                    dst[(s,d,*lead,r,c)]=part.astype(bf)
+            self.t1[s]=sum(came(self.a2r),plane(t.xyz[a]))
+            for d,to in enumerate(t.ring[b]): self.bs[s,d]=line(to).astype(bf)
+        elif stage==4:
+            self.t2[s]=sum(came(self.br),line(t.xyz[b]))
+            for d,to in enumerate(t.ring[first]): self.cs[s,d]=self.t2[s,to].astype(bf)
         elif stage==5:
-            self.t2[s]=line(t.xyz[b])+self.b2r[s,0].astype(f32)+self.b2r[s,1].astype(f32)
-            for d,to in enumerate(t.ring[first]):
-                self.cs[s,d]=self.t2[s,to].astype(bf)
-        elif stage==6:
-            v=self.t2[s,t.xyz[first]]
-            for d in range(3): v=v+self.cr[s,d].astype(f32)
-            self.out(column,v.astype(bf))
-        if stage<6:
+            self.out(column,sum(came(self.cr),self.t2[s,t.xyz[first]]).astype(bf))
+        if stage<5:
             for cp in self.copies(stage,i): cp.start()
 
 def split(core,v0,v1):
@@ -484,11 +491,11 @@
         return carry
     lax.fori_loop(0,L*B_STEPS,step,0)
     for r in range(TILES): store_dx(r).wait()
-    od[...]=odp[:,0:ROWS,:]
+    for l in range(L): od[:,l,:]=odp[l,0:ROWS,:]
 
 def backward(x,dy,h1,ga,gb,pt,at_,wc,gg,gu):
     return pl.pallas_call(b_kernel,
-        out_shape=[S((M,D),bf),S((L,R8,F),bf),S((L,R8,F),bf),S((L,ROWS,D),bf)]+[S((NG,M,COLS),bf)]*2,
+        out_shape=[S((M,D),bf),S((L,R8,F),bf),S((L,R8,F),bf),S((ROWS,L,D),bf)]+[S((NG,M,COLS),bf)]*2,
         in_specs=[ANY]*10,out_specs=[ANY]+[INVMEM]*3+[ANY]*2,
         scratch_shapes=[VMEM((L,PAD,D),bf),VMEM((M,D),bf),VMEM((D,M),bf),VMEM((TILES*F,COLS),bf),VMEM((2,2,M,COLS),f32),VMEM((2,2,M,COLS),bf),
             VMEM((2,COLS,D),bf),VMEM((2,2,NG,BM,COLS),bf),VMEM((2,BM,D),bf),
@@ -496,12 +503,34 @@
             +Scatter.scratch(R8,COLS,HALF_COLS)*2+Scatter.scratch(PAD,LANES,HALF_ROWS,6,4),
         compiler_params=params(1,63),name="backward")(x,dy,h1,ga,gb,pt,at_,wc,gg,gu)
 
+def finish_kernel(*refs):
+    n=len(refs)//4
+    src,dst,held,sems=(refs[k*n:k*n+n] for k in range(4))
+    def parts(r):
+        size=r.shape[0]//4 if r.shape[0]==M else r.shape[0]
+        return [pl.ds(k,size) for k in range(0,r.shape[0],size)]
+    jobs=[(m,k,p) for m in range(n) for k,p in enumerate(parts(src[m]))]
+    load=lambda m,k,p: pltpu.make_async_copy(src[m].at[p],held[m].at[p],sems[m].at[0,k])
+    store=lambda m,k,p: pltpu.make_async_copy(held[m].at[p],dst[m].at[p],sems[m].at[1,k])
+    for job in jobs: load(*job).start()
+    for job in jobs:
+        load(*job).wait()
+        store(*job).start()
+    for job in jobs: store(*job).wait()
+
+def finish(*arrays):
+    n=len(arrays)
+    return pl.pallas_call(finish_kernel,out_shape=[S(t.shape,t.dtype) for t in arrays],in_specs=[ANY]*n,out_specs=[ANY]*n,
+        scratch_shapes=[VMEM(t.shape,t.dtype) for t in arrays]+[DMA((2,4))]*n,
+        compiler_params=pltpu.CompilerParams(vmem_limit_bytes=62<<20),name="finish")(*arrays)
+
 def step(x,dy,wg,wu,wd):
     x,dy=x[0],dy[0]
-    gg,gu,_,ga,gb,pt,at_,h1,wc=forward(x,wg,wu,wd)
+    gg,gu,_,ga,gb,pt,at_,h1,wc=forward(x,wg,wu,jnp.swapaxes(wd,0,1))
     gg,gu=(t.reshape(ITEMS*D,COLS) for t in (gg,gu))
     dx,og,ou,od,_,_=backward(x,dy,h1,ga,gb,pt.reshape(L*TILES*F,COLS),at_,wc,gg,gu)
-    return dx[None],og,ou,od
+    dx,og,ou,od=finish(dx,og,ou,od)
+    return dx[None],og,ou,jnp.swapaxes(od,0,1)
 
 def solution(mesh):
     tok=P(("rep","dp"),None,None)

time: 360 us -> 349 us (0.969)
  local copies, waits for them, and re-layouts: 10.9 us -> 0 us
    unnamed x5 -> x0, local copies, waits for them, and re-layouts: 10.9 us -> none
    pallas_call x1, Pallas kernels: 136 us -> 128 us  [forward(): pl.pallas_call(f_kernel, out_shape=[S((ITEMS, *TORUS, R8, COLS), bf)] * 2...]
    pallas_call x1, Pallas kernels: 212 us -> 216 us  [backward(): pl.pallas_call(b_kernel, out_shape=[S((M, D), bf), S((L, R8, F), bf), S((...]
where the time goes in v4:
time: 349 us
  Pallas kernels  348 us (100%)
    pallas_call x1, Pallas kernels, backward(): pl.pallas_call(b_kernel, out_shape=[S((M, D), bf), S((L, R8, F), bf), S((...  216 us
    pallas_call x1, Pallas kernels, forward(): pl.pallas_call(f_kernel, out_shape=[S((ITEMS, *TORUS, R8, COLS), bf)] * 2...  128 us

profile of v4, /device:TPU:0, one launch (start us, length us, event | category | flops | bytes accessed | tf_op | source)
XLA Modules:
  0.0 348.6 jit_solution(8040906515940076633)
XLA Ops:
  0.6 127.8 %forward.1 = (bf16[22,4,4,4,2,8,256]{6,5,4,3,2,1,0:T(8,128)(2,1)}, bf16[22,4,4,4,2,8,256]{6,5,4,3,2,1,0:T(8,128)(2,1)}, bf16[16,4,4,4,2,24,128]{6,5,4,3,2,1,0:T(...) custom-call(bf16[2048,1024]{1,0:T(8,128)(2,1)} %bitcast.9, ...), custom_call_target="tpu_custom_call" | custom-call | tf_op jit(solution)/shard_map/forward/pallas_call | solution.py:255
  128.5 216.4 %backward.1 = (bf16[2048,1024]{1,0:T(8,128)(2,1)}, bf16[2,8,2816]{2,1,0:T(8,128)(2,1)}, bf16[2,8,2816]{2,1,0:T(8,128)(2,1)}, bf16[22,2,1024]{2,1,0:T(2,128)(2,1)...) custom-call(bf16[2048,1024]{1,0:T(8,128)(2,1)} %bitcast.10, bf16[2048,1024]{1,0:T(8,128)(2,1)} %bitcast.13, ...), custom_call_target="tpu_custom_call" | custom-call | tf_op jit(solution)/shard_map/backward/pallas_call | solution.py:497
  344.8 3.6 %finish.1 = (bf16[2048,1024]{1,0:T(8,128)(2,1)}, bf16[2,8,2816]{2,1,0:T(8,128)(2,1)}, bf16[2,8,2816]{2,1,0:T(8,128)(2,1)}, bf16[22,2,1024]{2,1,0:T(2,128)(2,1)}) custom-call(bf16[2048,1024]{1,0:T(8,128)(2,1)} %get-tuple-element.28.refs_0_, bf16[2,8,2816]{2,1,0:T(8,128)(2,1)} %get-tuple-element.29.refs_1_, bf16[2,8,2816]{2,1,0:T(8,128)(2,1)} %get-tuple-element.30.refs_2_, ...), custom_call_target="tpu_custom_call" | custom-call | tf_op jit(solution)/shard_map/finish/pallas_call | solution.py:523

commit v5 on v4

--- a/solution.py
+++ b/solution.py
@@ -23,7 +23,7 @@
 ITEMS=L*NG
 BM=256
 TILES=M//BM
-ORDERS=((2,1,0),(0,2,1),(1,0,2))
+ORDERS=((2,1,0),(2,0,1),(1,0,2))
 HALF_COLS=((pl.ds(0,R8),pl.ds(0,LANES)),(pl.ds(0,R8),pl.ds(LANES,LANES)))
 HALF_ROWS=((pl.ds(0,16),pl.ds(0,LANES)),(pl.ds(16,8),pl.ds(0,LANES)))
 DMA=pltpu.SemaphoreType.DMA
@@ -82,41 +82,43 @@
 
 
 SLOTS=4
+G_STAGES=("block","line","plane","pass plane","core","end")
+D_STAGES=("block","near line","pass line","plane","pass plane","core","end")
+COPIES={"block":3,"line":3,"near line":2,"pass line":2,"plane":2,"pass plane":2,"core":1,"end":0}
 G_OFF=(0,2,4,6,8,9)
-G_LAST=len(G_OFF)-1
+D_OFF=(0,2,4,6,8,10,11)
 G_DEPTH=G_OFF[-1]
+D_START=(2,2+ND+2)
 DM=TILES//2*BM
 DOWN_STEPS=M//DM
 F_STEPS=ITEMS+DOWN_STEPS
 
 class Gather:
-    COPIES=11
-    def __init__(self,torus,order,g,own,shards,halves,sems,local):
-        self.t,self.order,self.g,self.own,self.shards,self.halves,self.sems,self.local=torus,order,g,own,shards,halves,sems,local
+    def __init__(self,torus,order,stages,g,own,shards,halves,sems,local):
+        self.t,self.order,self.stages,self.g,self.own,self.shards,self.halves,self.sems,self.local=torus,order,stages,g,own,shards,halves,sems,local
     def region(self,i,full,axis=None,v=None,part=(ALL,ALL)):
         where=(ALL if k in full else v if k==axis else self.t.xyz[k] for k in range(3))
         return self.g.at[(i,*where,self.t.c,*part)]
     def pieces(self,stage,i):
         t=self.t
         a,b,last=self.order
-        if stage==0:
+        kind=self.stages[stage]
+        if kind=="block":
             mine=self.region(i,())
             return [(self.own(i),mine,to) for to in t.ringid[a]]
-        if stage==1:
-            mine=self.region(i,(a,))
-            return [(mine,mine,to) for to in t.ringid[b]]
-        if stage==4:
+        if kind=="core":
             mine=self.region(i,(0,1,2))
             return [(mine,mine,t.partner)]
-        to=(t.pid[last],t.qid[last])
-        if stage==2:
-            mine=self.region(i,(a,b))
-            return [(mine,mine,to[d]) for d in range(2)]
-        came=(t.q[last],t.p[last])
-        parts=[self.region(i,(a,b),last,came[d],self.halves[d]) for d in range(2)]
-        return [(parts[d],parts[d],to[d]) for d in range(2)]
+        axis,full=(last,(a,b)) if kind.endswith("plane") else (b,(a,))
+        to=t.ringid[axis] if kind=="line" else (t.pid[axis],t.qid[axis])
+        if kind.startswith("pass"):
+            came=(t.q[axis],t.p[axis])
+            parts=[self.region(i,full,axis,came[d],self.halves[d]) for d in range(2)]
+            return [(parts[d],parts[d],to[d]) for d in range(2)]
+        mine=self.region(i,full)
+        return [(mine,mine,dev) for dev in to]
     def copies(self,stage,i,slot):
-        first=(0,3,6,8,10)[stage]
+        first=sum(COPIES[k] for k in self.stages[:stage])
         send,recv=self.sems
         return [pltpu.make_async_remote_copy(src_ref=src,dst_ref=dst,send_sem=send.at[first+k],recv_sem=recv.at[slot,first+k],
             device_id={"dp":to},device_id_type=MESH) for k,(src,dst,to) in enumerate(self.pieces(stage,i))]
@@ -127,13 +129,13 @@
         if stage>0:
             for cp in self.copies(stage-1,i,slot): cp.wait_recv()
             if stage==1: self.own_copy(i,slot).wait()
-        if stage<G_LAST:
+        if stage<len(self.stages)-1:
             for cp in self.copies(stage,i,slot): cp.start()
             if stage==0: self.own_copy(i,slot).start()
     def drain(self):
         self.own=lambda i: self.shards
-        for stage in range(G_LAST):
-            for k,cp in enumerate(self.copies(stage,ALL,0)): cp.wait_send()
+        for stage in range(len(self.stages)-1):
+            for cp in self.copies(stage,ALL,0): cp.wait_send()
 
 def f_kernel(x,wg,wu,wd,gg,gu,gd,ga,gb,pt,at_,h1,wc,
         wdp,xv,av,ptv,wcv,wv,dv,abv,atv,hv,xsem,wsem,dsem,absem,ptsem,atsem,hsem,wcsem,*gsems):
@@ -147,9 +149,9 @@
     own_g=lambda i: wg.at[lax.div(i,NG),:,aligned(lax.rem(i,NG),COLS)]
     own_u=lambda i: wu.at[lax.div(i,NG),:,aligned(lax.rem(i,NG),COLS)]
     own_d=lambda k: wdp.at[lax.div(k,ND),:,aligned(lax.rem(k,ND),LANES)]
-    eg=Gather(torus,ORDERS[0],gg,own_g,wg,HALF_COLS,gsems[0:2],gsems[2])
-    eu=Gather(torus,ORDERS[1],gu,own_u,wu,HALF_COLS,gsems[3:5],gsems[5])
-    ed=Gather(torus,ORDERS[2],gd,own_d,wdp,HALF_ROWS,gsems[6:8],gsems[8])
+    eg=Gather(torus,ORDERS[0],G_STAGES,gg,own_g,wg,HALF_COLS,gsems[0:2],gsems[2])
+    eu=Gather(torus,ORDERS[1],G_STAGES,gu,own_u,wu,HALF_COLS,gsems[3:5],gsems[5])
+    ed=Gather(torus,ORDERS[2],D_STAGES,gd,own_d,wdp,HALF_ROWS,gsems[6:8],gsems[8])
     def load_d(k):
         return pltpu.make_async_copy(gd.at[k],dv.at[lax.rem(k,2)],dsem.at[lax.rem(k,2)])
     def store_wc(l):
@@ -164,19 +166,22 @@
         lax.fori_loop(0,RING,plane,0)
         @pl.when(lax.rem(k,ND)==ND-1)
         def _(): store_wc(lax.div(k,ND)).start()
+    def when_down(u,run):
+        second=(u>=D_START[1])&(u<D_START[1]+ND)
+        @pl.when(((u>=D_START[0])&(u<D_START[0]+ND))|second)
+        def _(): run(u-jnp.where(u>=D_START[1],D_START[1]-ND,D_START[0]))
+    def run_down(stage,k):
+        ed.run(stage,k)
+        if stage==len(D_STAGES)-1: load_d(k).start()
     def tick(t):
-        i=t-G_DEPTH-1
-        @pl.when((i>=0)&(i<L*ND))
-        def _(): compact(i)
-        for stage in reversed(range(G_LAST+1)):
+        when_down(t-D_OFF[-1]-1,compact)
+        for stage in reversed(range(len(D_STAGES))):
+            when_down(t-D_OFF[stage],functools.partial(run_down,stage))
+        for stage in reversed(range(len(G_STAGES))):
             i=t-G_OFF[stage]
             @pl.when((i>=0)&(i<ITEMS))
             def _():
                 eg.run(stage,i); eu.run(stage,i)
-                @pl.when(i<L*ND)
-                def _():
-                    ed.run(stage,i)
-                    if stage==G_LAST: load_d(i).start()
     item_of=lambda k: jnp.where(k<NG,k,k-DOWN_STEPS)
     is_item=lambda k: ((k>=0)&(k<NG))|((k>=NG+DOWN_STEPS)&(k<F_STEPS))
     def load_w(i):
@@ -258,13 +263,13 @@
         in_specs=[ANY]+[INVMEM]*3,out_specs=[ANY]*9,
         scratch_shapes=[VMEM((L,PAD,D),bf),VMEM((M,D),bf),VMEM((M,D),bf),VMEM((TILES,F,BM),bf),VMEM((L,F,D),bf),VMEM((2,2,*TORUS,R8,COLS),bf),
             VMEM((2,*TORUS,PAD,LANES),bf),VMEM((2,2,M,COLS),f32),VMEM((DOWN_STEPS,D,DM),bf),VMEM((DOWN_STEPS,DM,D),bf),
-            DMA,DMA((2,2)),DMA((2,)),DMA((2,2)),DMA((2,)),DMA((DOWN_STEPS,)),DMA((DOWN_STEPS,)),DMA((L,))]+[DMA((Gather.COPIES,)),DMA((SLOTS,Gather.COPIES)),DMA((SLOTS,))]*3,
+            DMA,DMA((2,2)),DMA((2,)),DMA((2,2)),DMA((2,)),DMA((DOWN_STEPS,)),DMA((DOWN_STEPS,)),DMA((L,))]+[DMA((n,)) if k==0 else DMA((SLOTS,n)) if k==1 else DMA((SLOTS,)) for stages in (G_STAGES,G_STAGES,D_STAGES) for n in (sum(COPIES[k] for k in stages),) for k in range(3)],
         compiler_params=params(0,62),name="forward")(x,wg,wu,wd)
 
 
 B_TAIL=NG+1
 B_STEPS=B_TAIL+TILES
-SEND,DOWN=2,2
+SEND,DOWN=2,3
 S_STAGES=6
 
 class Scatter:
@@ -406,10 +411,13 @@
                 e.own[o,k]=own.reshape(RING,RING,R8,COLS)
                 e.ds[to,k]=other.astype(bf).reshape(RING,RING,R8,COLS)
     def grad_down(half,k):
-        dh=dhv[:,aligned(lax.div(k,2),COLS)]
-        first=half*ND+k
-        for g in range(RING*RING):
-            rows=jnp.concatenate([both[pl.ds(r*F+g*GROUP,GROUP),:] for r in range(TILES)],1)
+        pair,part=lax.div(k,2),lax.rem(k,2)
+        dh=dhv[:,aligned(pair,COLS)]
+        item=half*ND+2*pair
+        for g in range(EIGHT):
+            x,y=part*2+g//RING,g%RING
+            first=(x*RING+y)*GROUP
+            rows=jnp.concatenate([both[pl.ds(pl.multiple_of(r*F+first,PAD-EIGHT),GROUP),:] for r in range(TILES)],1)
             v=dot(rows,dh)
             for z in range(RING):
                 pair=[v[ROWS*d:ROWS*d+ROWS] for d in (2*z,2*z+1)]
@@ -417,8 +425,8 @@
                 other=other.astype(bf)
                 for e in range(2):
                     cols=slice(e*LANES,e*LANES+LANES)
-                    ed.own[Scatter.slot(ed.own,first+e),g//RING,g%RING,z,0:ROWS,:]=own[:,cols]
-                    ed.ds[Scatter.slot(ed.ds,first+e),g//RING,g%RING,z,0:ROWS,:]=other[:,cols]
+                    ed.own[Scatter.slot(ed.own,item+e),x,y,z,0:ROWS,:]=own[:,cols]
+                    ed.ds[Scatter.slot(ed.ds,item+e),x,y,z,0:ROWS,:]=other[:,cols]
     def grad_h(half,r):
         s=lax.rem(r,2)
         acc=None
@@ -440,18 +448,17 @@
         half,s=lax.div(now,B_STEPS),lax.rem(now,B_STEPS)
         r=s-B_TAIL
         tick(half,s)
-        @pl.when(s==0)
-        def _(): each(load_pt(half),True)
         @pl.when(s<NG-1)
         def _(): each(prefetch(half,s+1),True)
-        @pl.when(s==DOWN+ND)
-        def _(): each(load_w(half),True)
+        @pl.when(s==1)
+        def _(): each(load_pt(half),True)
         @pl.when(s==B_TAIL-1)
         def _():
             each(store_gs(NG-1),False)
             each(store_gs(NG-2),False)
             each(load_tile(0),True)
             load_h(half,0,True)
+            each(load_w(half),True)
         @pl.when(s==B_TAIL)
         def _(): each(load_w(half),False)
         @pl.when((s==B_TAIL)&(half<L-1))
@@ -475,13 +482,14 @@
         def _():
             each(load_tile(r),False)
             load_h(half,r,False)
-        @pl.when((s>=DOWN)&(s<DOWN+ND)&(lax.rem(s,2)==0))
-        def _(): grad_down(half,s-DOWN)
         @pl.when(s==0)
         def _(): front(s)
-        @pl.when((s>0)&(s<NG))
+        @pl.when((s>0)&(s<DOWN))
         def _():
             front(s); back(half,s-1)
+        @pl.when((s>=DOWN)&(s<NG))
+        def _():
+            front(s); grad_down(half,s-DOWN); back(half,s-1)
         @pl.when(s==NG)
         def _(): back(half,s-1)
         @pl.when(s<NG)

time: 349 us -> 328 us (0.940)
  Pallas kernels: 348 us -> 328 us
    pallas_call x1, Pallas kernels: 216 us -> 201 us  [backward(): pl.pallas_call(b_kernel, out_shape=[S((M, D), bf), S((L, R8, F), bf), S((...]
    pallas_call x1, Pallas kernels: 128 us -> 123 us  [forward(): pl.pallas_call(f_kernel, out_shape=[S((ITEMS, *TORUS, R8, COLS), bf)] * 2...]
where the time goes in v5:
time: 328 us
  Pallas kernels  328 us (100%)
    pallas_call x1, Pallas kernels, backward(): pl.pallas_call(b_kernel, out_shape=[S((M, D), bf), S((L, R8, F), bf), S((...  201 us
    pallas_call x1, Pallas kernels, forward(): pl.pallas_call(f_kernel, out_shape=[S((ITEMS, *TORUS, R8, COLS), bf)] * 2...  123 us

profile of v5, /device:TPU:0, one launch (start us, length us, event | category | flops | bytes accessed | tf_op | source)
XLA Modules:
  0.0 328.3 jit_solution(445488709041471124)
XLA Ops:
  0.6 122.9 %forward.1 = (bf16[22,4,4,4,2,8,256]{6,5,4,3,2,1,0:T(8,128)(2,1)}, bf16[22,4,4,4,2,8,256]{6,5,4,3,2,1,0:T(8,128)(2,1)}, bf16[16,4,4,4,2,24,128]{6,5,4,3,2,1,0:T(...) custom-call(bf16[2048,1024]{1,0:T(8,128)(2,1)} %bitcast.9, ...), custom_call_target="tpu_custom_call" | custom-call | tf_op jit(solution)/shard_map/forward/pallas_call | solution.py:260
  123.5 201.0 %backward.1 = (bf16[2048,1024]{1,0:T(8,128)(2,1)}, bf16[2,8,2816]{2,1,0:T(8,128)(2,1)}, bf16[2,8,2816]{2,1,0:T(8,128)(2,1)}, bf16[22,2,1024]{2,1,0:T(2,128)(2,1)...) custom-call(bf16[2048,1024]{1,0:T(8,128)(2,1)} %bitcast.10, bf16[2048,1024]{1,0:T(8,128)(2,1)} %bitcast.13, ...), custom_call_target="tpu_custom_call" | custom-call | tf_op jit(solution)/shard_map/backward/pallas_call | solution.py:505
  324.6 3.6 %finish.1 = (bf16[2048,1024]{1,0:T(8,128)(2,1)}, bf16[2,8,2816]{2,1,0:T(8,128)(2,1)}, bf16[2,8,2816]{2,1,0:T(8,128)(2,1)}, bf16[22,2,1024]{2,1,0:T(2,128)(2,1)}) custom-call(bf16[2048,1024]{1,0:T(8,128)(2,1)} %get-tuple-element.28.refs_0_, bf16[2,8,2816]{2,1,0:T(8,128)(2,1)} %get-tuple-element.29.refs_1_, bf16[2,8,2816]{2,1,0:T(8,128)(2,1)} %get-tuple-element.30.refs_2_, ...), custom_call_target="tpu_custom_call" | custom-call | tf_op jit(solution)/shard_map/finish/pallas_call | solution.py:531
